TPU v7x, 256 devices: a 4x2x16 block of a 4x16x16 slice. The times are simulated.
256 devices in a mesh: rep: 2 (over y), gx: 128 (over z, x, core).
Axes of the slice: x: 4, y: 2, z: 16, core: 2. Of those that a mesh axis runs over, the one named last changes fastest.
The devices are a block of a 4x16x16 slice.
Arguments:
- positions: float32 [3, 393216], P(None, ('rep', 'gx')), parts along dimension 1, may hold values from 0 to 768
- velocities: float32 [3, 393216], P(None, ('rep', 'gx')), parts along dimension 1, may hold values from -9 to 9
- atom_params: float32 [4, 393216], P(None, ('rep', 'gx')), parts along dimension 1, may hold values from -1 to 2, as said below
- pair_list: int32 [3, 4325376], P(None, ('rep', 'gx')), parts along dimension 1, may hold values from 0 to 479, as said below
- pair_count: int32 [256], P(('rep', 'gx')), parts along dimension 0, may hold values from 2112 to 16896, as said below
- exclusion: int32 [4, 4325376], P(None, ('rep', 'gx')), parts along dimension 1, may hold values from 0 to 65535, as said below
- halo_far: int32 [24576], P(('rep', 'gx')), parts along dimension 0, may hold values from 0 to 191, as said below
- box_lengths: float32 [6], P('rep'), parts along dimension 0, may hold values from 12 to 768
- extended_variables: float32 [8], P('rep'), parts along dimension 0, may hold values from -0.3 to 0.3
Outputs:
- forces: float32 [3, 393216], P(None, ('rep', 'gx')), parts along dimension 1
- new_velocities: float32 [3, 393216], P(None, ('rep', 'gx')), parts along dimension 1
- new_positions: float32 [3, 393216], P(None, ('rep', 'gx')), parts along dimension 1
- new_coupling: float32 [8], P('rep'), parts along dimension 0
There are 2 independent parts, one for each index of `rep`. A program takes and returns all parts, laid end to end along the dimension named above; each array names one. Nothing has to cross between parts.
Inputs may be any that keep to these rules, and one draw needn't show every extreme that they name: `pair_list`: row 0 is a local cluster 0 to 191, row 1 a slot 0 to 479 of the slot table, row 2 an image code 0 to 8. Over each domain's used columns row 0 never falls (the list is grouped by its first cluster). Unused columns hold valid entries too. `pair_count`: at most 16896; some domain uses all 16896 columns in every draw. `exclusion`: each word holds 16 bits; bit 1 means the atom pair interacts. `halo_far`: 96 distinct local clusters of each domain. `atom_params`: rows 1 to 3 are positive.
All inputs are finite; a program needn't handle non-finite values.
Results may differ from a plain program's by a relative error of at most 0.0003.
Values sent between devices are 32-bit elements; how exact they have to be, the bound alone decides.
A program may use at most 64 MiB of HBM per device.

v0:
```python
import functools

import jax
import jax.numpy as jnp
from jax import lax
from jax.sharding import Mesh
from jax.sharding import PartitionSpec as P

LY = 12
GX = ("gx_0", "gx_1", "gx_2")
REP_GX = ("rep", "gx_0", "gx_1", "gx_2")


time_step = 0.25
reaction_term = 1.0 / 1331.0
thermal_scale_unit = 2.0
reservoir_inertia_mass = 4.0
barostat_gain = 0.1
pressure_target = 1.0


def over_axes(array, axes):
    return functools.reduce(lax.psum, axes, array)


def passed_along(value, axis, steps):
    count = lax.axis_size(axis)
    pairs = [(source, (source + steps) % count) for source in range(count)]
    return lax.ppermute(value, axis, pairs)


def pair_tiles(slot_table, pair_rows, word_rows, usable, box_lengths):
    tile_width = pair_rows.shape[1]
    first_rows = jnp.take(slot_table, pair_rows[0], axis=0).T.reshape(6, 8, tile_width)
    second_rows = jnp.take(slot_table, pair_rows[1], axis=0).T.reshape(6, 8, tile_width)
    image_y = (pair_rows[2] // 3 - 1).astype(jnp.float32) * box_lengths[1]
    image_z = (pair_rows[2] % 3 - 1).astype(jnp.float32) * box_lengths[2]
    delta_x = second_rows[0][None, :, :] - first_rows[0][:, None, :]
    delta_y = second_rows[1][None, :, :] - first_rows[1][:, None, :] + image_y
    delta_z = second_rows[2][None, :, :] - first_rows[2][:, None, :] + image_z
    shifts = (jnp.arange(64, dtype=jnp.int32) % 16)[:, None]
    mask_bits = jnp.right_shift(jnp.repeat(word_rows, 16, axis=0), shifts) & 1
    interact = (mask_bits.reshape(8, 8, tile_width) == 1) & usable[None, None, :]
    radius_sq = delta_x * delta_x + delta_y * delta_y + delta_z * delta_z
    radius_sq = jnp.where(interact, radius_sq, 1.0)
    inverse = lax.rsqrt(radius_sq)
    inverse_sq = inverse * inverse
    inverse_six = inverse_sq * inverse_sq * inverse_sq
    charge_pair = first_rows[3][:, None, :] * second_rows[3][None, :, :]
    dispersion = first_rows[4][:, None, :] * second_rows[4][None, :, :]
    repulsion = first_rows[5][:, None, :] * second_rows[5][None, :, :]
    scalar = (
        charge_pair * (inverse * inverse_sq - reaction_term)
        + (12.0 * repulsion * inverse_six - 6.0 * dispersion) * inverse_six * inverse_sq
    )
    scalar = jnp.where(interact, scalar, 0.0)
    components = (delta_x, delta_y, delta_z)
    onto_second = jnp.stack([jnp.sum(scalar * component, axis=0) for component in components])
    onto_first = -jnp.stack([jnp.sum(scalar * component, axis=1) for component in components])
    virial = -0.5 * jnp.stack([jnp.sum(scalar * component * component) for component in components])
    tile_terms = jnp.concatenate(
        [onto_first.reshape(24, tile_width), onto_second.reshape(24, tile_width)], axis=1
    ).T
    owners = jnp.concatenate([pair_rows[0], pair_rows[1]])
    return (tile_terms, owners, virial)


def on_device(
    positions,
    velocities,
    atom_params,
    pair_list,
    pair_count,
    exclusion,
    halo_far,
    box_lengths,
    extended_variables,
):
    atoms_here = positions.shape[1]
    clusters = atoms_here // 8
    far_clusters = halo_far.shape[0]
    slots = 2 * clusters + far_clusters
    block_rows = pair_list.shape[1] // LY
    domain_index = lax.axis_index(GX)
    axis_count = lax.axis_size(GX)
    inverse_mass = atom_params[3]
    kinetic = 0.5 * jnp.sum(velocities * velocities / inverse_mass[None, :], axis=1)
    overall_motion_work = over_axes(kinetic, GX)
    packed = jnp.concatenate([positions, atom_params[:3]], axis=0)
    far_rows = packed.reshape(6, clusters, 8)[:, halo_far, :].reshape(6, far_clusters * 8)
    near_rows = passed_along(packed, GX, -1)
    far_in = passed_along(far_rows, GX, -2)
    near_rows = near_rows.at[0].add(jnp.where(domain_index == axis_count - 1, box_lengths[0], 0.0))
    far_in = far_in.at[0].add(jnp.where(domain_index >= axis_count - 2, box_lengths[0], 0.0))
    slot_table = jnp.concatenate([packed, near_rows, far_in], axis=1)
    slot_table = slot_table.reshape(6, slots, 8).transpose(1, 0, 2).reshape(slots, 48)
    pair_total = pair_count[0]
    slot_numbers = jnp.arange(slots, dtype=jnp.int32)[:, None]

    def one_block(block_index, running):
        accumulated, virial = running
        first_row = block_index * block_rows
        pair_block = lax.dynamic_slice_in_dim(pair_list, first_row, block_rows, 1)
        word_block = lax.dynamic_slice_in_dim(exclusion, first_row, block_rows, 1)
        usable = first_row + jnp.arange(block_rows, dtype=jnp.int32) < pair_total
        tile_terms, owners, partial_value = pair_tiles(
            slot_table, pair_block, word_block, usable, box_lengths
        )
        selector = (slot_numbers == owners[None, :]).astype(jnp.float32)
        accumulated = accumulated + jnp.dot(
            selector,
            tile_terms,
            precision=lax.Precision.HIGHEST,
            preferred_element_type=jnp.float32,
        )
        return (accumulated, virial + partial_value)

    block_count = (pair_total + block_rows - 1) // block_rows
    start_state = (jnp.zeros((slots, 24), jnp.float32), jnp.zeros((3,), jnp.float32))
    accumulated, virial = lax.fori_loop(0, block_count, one_block, start_state)
    columns = accumulated.T
    near_back = passed_along(columns[:, clusters : 2 * clusters], GX, 1)
    far_back = passed_along(columns[:, 2 * clusters :], GX, 2)
    summed = columns[:, :clusters] + near_back
    summed = summed.at[:, halo_far].add(far_back)
    forces = summed.reshape(3, 8, clusters).transpose(0, 2, 1).reshape(3, atoms_here)
    virial_total = over_axes(virial, GX)
    combined_potential = jnp.sum(overall_motion_work)
    particle_number_overall = atoms_here * axis_count
    volume = box_lengths[0] * box_lengths[1] * box_lengths[2]
    thermal_ratio_value = (
        2.0 * combined_potential / (3.0 * particle_number_overall * thermal_scale_unit)
    )
    reservoir_damping = extended_variables[0] + reservoir_inertia_mass * (thermal_ratio_value - 1.0)
    box_rates = extended_variables[1:] + barostat_gain * (
        overall_motion_work - virial_total - pressure_target * volume / 2.0
    ) / (combined_potential / 3.0)
    new_velocities = velocities + time_step * (
        forces * inverse_mass[None, :] - (reservoir_damping + box_rates[:, None]) * velocities
    )
    new_positions = positions * (1.0 + time_step * box_rates[:, None]) + time_step * new_velocities
    new_coupling = jnp.concatenate([reservoir_damping[None], box_rates])
    return (forces, new_velocities, new_positions, new_coupling)


def solution(mesh):
    finer = Mesh(mesh.devices.reshape(mesh.shape["rep"], 16, 4, 2), ("rep", "gx_0", "gx_1", "gx_2"))
    placed = (
        P(None, REP_GX),
        P(None, REP_GX),
        P(None, REP_GX),
        P(None, REP_GX),
        P(REP_GX),
        P(None, REP_GX),
        P(REP_GX),
        P("rep"),
        P("rep"),
    )
    return jax.shard_map(
        on_device,
        mesh=finer,
        in_specs=placed,
        out_specs=(P(None, REP_GX), P(None, REP_GX), P(None, REP_GX), P("rep")),
        check_vma=False,
    )
```

profile of v0, /device:TPU:40, one launch (start us, length us, event | category | flops | bytes accessed | tf_op | source)
XLA Modules:
  0.0 497.9 jit_solution(10788606077927367968)
XLA Ops:
  1.4 24.6 %collective-permute-start = (f32[6,1536]{1,0:T(8,128)S(1)}, f32[6,1536]{1,0:T(8,128)S(1)}, u32[]{:S(2)}, u32[]{:S(2)}) collective-permute-start(f32[6,1536]{1,0:T(8,128)S(1)} %pad_maximum_fusion.1), channel_id=1, source_target_pairs={{0,127},{1,0},{2,1},{3,2},{4,3},{5,4},{6,5},{7,6},{8,7},{9,8},{10,... | collective-permute-start | bytes 110600 | tf_op jit(solution)/shard_map/ppermute | solution.py:29
  38.1 204.4 %while.18 = (s32[]{:T(128)}, f32[480,24]{0,1:T(8,128)}, f32[3]{0:T(128)}, s32[]{:T(128)}, s32[3,16896]{1,0:T(4,128)}, /*index=5*/s32[4,16896]{1,0:T(4,128)}, s32...) while((s32[]{:T(128)}, f32[480,24]{0,1:T(8,128)}, ...), condition=%wide.region_10.12_spmd.clone, body=%wide.region_0.11_spmd.clone.sunk | while | flops 397501280 | bytes 8990699 | solution.py:120
  45.3 2.7 gather_fusion.1
  48.2 2.7 gather_fusion
  51.2 2.3 fusion.58
  58.2 2.3 fusion.59
  69.0 2.5 fusion.65
  79.3 2.7 gather_fusion.1
  82.3 2.7 gather_fusion
  92.3 2.3 fusion.59
  103.0 2.5 fusion.65
  113.5 2.7 gather_fusion.1
  116.4 2.7 gather_fusion
  126.4 2.3 fusion.59
  137.1 2.5 fusion.65
  147.5 2.7 gather_fusion.1
  150.5 2.7 gather_fusion
  160.5 2.3 fusion.59
  171.2 2.5 fusion.65
  181.6 2.7 gather_fusion.1
  184.5 2.7 gather_fusion
  194.5 2.3 fusion.59
  205.3 2.5 fusion.65
  215.6 2.7 gather_fusion.1
  218.6 2.7 gather_fusion
  228.6 2.3 fusion.59
  239.3 2.5 fusion.65
  242.5 228.5 %all-reduce = (f32[3]{0:T(128)S(1)}, f32[3]{0:T(128)S(1)}) all-reduce(f32[3]{0:T(128)} %broadcast_multiply_fusion, f32[3]{0:T(128)} %get-tuple-element.500), channel_id=1, replica_groups=mesh['rep'=2,'gx_0'=16,'gx_1'=4,'gx_2'=2] {'gx_0'}, use_global_device_ids=true, to_apply=%region_13.15 | all-reduce | flops 6 | bytes 48 | tf_op jit(solution)/shard_map/psum | solution.py:23
  471.0 9.1 %all-reduce.1 = (f32[3]{0:T(128)S(1)}, f32[3]{0:T(128)S(1)}) all-reduce(f32[3]{0:T(128)S(1)} %get-tuple-element.283, f32[3]{0:T(128)S(1)} %get-tuple-element.284), channel_id=1, replica_groups=mesh['rep'=2,'gx_0'=16,'gx_1'=4,'gx_2'=2] {'gx_1'}, use_global_device_ids=true, to_apply=%region_14.16 | all-reduce | flops 6 | bytes 48 | tf_op jit(solution)/shard_map/psum | solution.py:23
  480.1 2.7 all-reduce.2
  488.5 4.5 collective-permute-done.2
  493.1 2.4 collective-permute-done.3
  (407 shorter events, 154.6 us)
Async XLA Ops:
  1.4 33.8 %collective-permute-start = (f32[6,1536]{1,0:T(8,128)S(1)}, f32[6,1536]{1,0:T(8,128)S(1)}, u32[]{:S(2)}, u32[]{:S(2)}) collective-permute-start(f32[6,1536]{1,0:T(8,128)S(1)} %pad_maximum_fusion.1), channel_id=1, source_target_pairs={{0,127},{1,0},{2,1},{3,2},{4,3},{5,4},{6,5},{7,6},{8,7},{9,8},{10,... | collective-permute-start | bytes 110600 | tf_op jit(solution)/shard_map/ppermute | solution.py:29
  27.6 7.8 %copy-start.4 = (f32[3,1536]{1,0:T(4,128)S(1)}, f32[3,1536]{1,0:T(4,128)}, u32[]{:S(2)}) copy-start(f32[3,1536]{1,0:T(4,128)} %param.17) | copy-start | bytes 55300
  28.9 6.2 %collective-permute-start.1 = (f32[6,768]{1,0:T(8,128)S(1)}, f32[6,768]{1,0:T(8,128)S(1)}, u32[]{:S(2)}, u32[]{:S(2)}) collective-permute-start(f32[6,768]{1,0:T(8,128)S(1)} %reshape.315), channel_id=1, source_target_pairs={{0,126},{1,127},{2,0},{3,1},{4,2},{5,3},{6,4},{7,5},{8,6},{9,7},{1... | collective-permute-start | bytes 55304 | tf_op jit(solution)/shard_map/ppermute | solution.py:29
  29.8 5.5 %copy-start.15 = (f32[1536]{0:T(1024)}, f32[1536]{0:T(1024)S(1)}, u32[]{:S(2)}) copy-start(f32[1536]{0:T(1024)S(1)} %slice_reduce_fusion) | copy-start | bytes 18436
  60.6 3.4 copy-start
  65.0 4.0 copy-start.3
  65.0 4.0 copy-start.7
  65.7 6.4 %copy-start.14 = (f32[3]{0:T(128)S(1)}, f32[3]{0:T(128)}, u32[]{:S(2)}) copy-start(f32[3]{0:T(128)} %get-tuple-element.513) | copy-start | bytes 40 | tf_op jit(solution)/shard_map/while
  94.6 3.4 copy-start
  99.0 4.0 copy-start.3
  99.1 4.0 copy-start.7
  99.8 6.4 %copy-start.14 = (f32[3]{0:T(128)S(1)}, f32[3]{0:T(128)}, u32[]{:S(2)}) copy-start(f32[3]{0:T(128)} %get-tuple-element.513) | copy-start | bytes 40 | tf_op jit(solution)/shard_map/while
  128.8 3.4 copy-start
  133.2 4.0 copy-start.3
  133.2 4.0 copy-start.7
  133.9 6.4 %copy-start.14 = (f32[3]{0:T(128)S(1)}, f32[3]{0:T(128)}, u32[]{:S(2)}) copy-start(f32[3]{0:T(128)} %get-tuple-element.513) | copy-start | bytes 40 | tf_op jit(solution)/shard_map/while
  162.8 3.4 copy-start
  167.2 4.0 copy-start.3
  167.2 4.0 copy-start.7
  168.0 6.4 %copy-start.14 = (f32[3]{0:T(128)S(1)}, f32[3]{0:T(128)}, u32[]{:S(2)}) copy-start(f32[3]{0:T(128)} %get-tuple-element.513) | copy-start | bytes 40 | tf_op jit(solution)/shard_map/while
  201.3 4.0 copy-start.3
  201.3 4.0 copy-start.7
  202.0 6.4 %copy-start.14 = (f32[3]{0:T(128)S(1)}, f32[3]{0:T(128)}, u32[]{:S(2)}) copy-start(f32[3]{0:T(128)} %get-tuple-element.513) | copy-start | bytes 40 | tf_op jit(solution)/shard_map/while
  230.9 3.4 copy-start
  235.4 4.0 copy-start.3
  235.4 4.0 copy-start.7
  236.1 6.4 %copy-start.14 = (f32[3]{0:T(128)S(1)}, f32[3]{0:T(128)}, u32[]{:S(2)}) copy-start(f32[3]{0:T(128)} %get-tuple-element.513) | copy-start | bytes 40 | tf_op jit(solution)/shard_map/while
  242.5 254.7 %copy-start.5 = (f32[3,1536]{1,0:T(4,128)S(1)}, f32[3,1536]{1,0:T(4,128)}, u32[]{:S(2)}) copy-start(f32[3,1536]{1,0:T(4,128)} %param.17) | copy-start | bytes 55300
  242.5 254.7 %copy-start.12 = (f32[3,1536]{1,0:T(4,128)S(1)}, f32[3,1536]{1,0:T(4,128)}, u32[]{:S(2)}) copy-start(f32[3,1536]{1,0:T(4,128)} %param.18) | copy-start | bytes 55300
  242.5 254.7 %copy-start.16 = (f32[1536]{0:T(1024)S(1)}, f32[1536]{0:T(1024)}, u32[]{:S(2)}) copy-start(f32[1536]{0:T(1024)} %copy-done.15) | copy-start | bytes 18436
  485.6 7.5 %collective-permute-start.2 = (f32[24,192]{0,1:T(8,128)S(1)}, f32[24,192]{0,1:T(8,128)S(1)}, u32[]{:S(2)}, u32[]{:S(2)}) collective-permute-start(f32[24,192]{0,1:T(8,128)S(1)} %slice.250), channel_id=1, source_target_pairs={{0,1},{1,2},{2,3},{3,4},{4,5},{5,6},{6,7},{7,8},{8,9},{9,10},{10,1... | collective-permute-start | bytes 55304 | tf_op jit(solution)/shard_map/ppermute | solution.py:29
  487.9 7.6 %collective-permute-start.3 = (f32[24,96]{0,1:T(8,128)S(1)}, f32[24,96]{0,1:T(8,128)S(1)}, u32[]{:S(2)}, u32[]{:S(2)}) collective-permute-start(f32[24,96]{0,1:T(8,128)S(1)} %slice.251), channel_id=1, source_target_pairs={{0,2},{1,3},{2,4},{3,5},{4,6},{5,7},{6,8},{7,9},{8,10},{9,11},{10,... | collective-permute-start | bytes 27656 | tf_op jit(solution)/shard_map/ppermute | solution.py:29
  (42 other events, 56.7 us)
where the time goes:
time: 500 us; the launch traced here: 498 us
  blocking collectives  240 us (48%)
  local copies, waits for them, and re-layouts  135 us (27%)
  other arithmetic  66.6 us (13%)
  starting transfers between devices  26.4 us (5%)
  matrix products  15 us (3%)
  waiting for transfers between devices  6.9 us (1%)
  between operations  6.79 us (1%)
    psum x3, blocking collectives, over_axes(): return functools.reduce(lax.psum, axes, array)  240 us
    slice x24, local copies, waits for them, and re-layouts, pair_tiles(): charge_pair = first_rows[3][:, None, :] * second_rows[3][None, :, :]  30.7 us
    ppermute x4, starting transfers between devices, passed_along(): return lax.ppermute(value, axis, pairs)  26.4 us
    slice x12, local copies, waits for them, and re-layouts, pair_tiles(): dispersion = first_rows[4][:, None, :] * second_rows[4][None, :, :]  20.1 us
    gather x6, local copies, waits for them, and re-layouts, pair_tiles(): jnp.take(slot_table, pair_rows[0], axis=0).T.reshape(6, 8, tile_width)  16.2 us
    gather x6, local copies, waits for them, and re-layouts, pair_tiles(): jnp.take(slot_table, pair_rows[1], axis=0).T.reshape(6, 8, tile_width)  16.2 us
    slice x12, local copies, waits for them, and re-layouts, pair_tiles(): delta_z = second_rows[2][None, :, :] - first_rows[2][:, None, :] + image_z  16 us
    dot_general x6, matrix products, one_block(): jnp.dot(selector, tile_terms, precision=lax.Precision.HIGHEST, preferred_...  15 us
  transfers between devices with their start and end apart: 4, of which 2 were waited for; matrix products, arithmetic and copies ran while one was open for 1% of the time, Pallas kernels for 0%

commit v1 on v0

v1 whole, which is shorter than its diff:
```python
import functools

import jax
import jax.numpy as jnp
from jax import lax
from jax.experimental import pallas as pl
from jax.experimental.pallas import tpu as pltpu
from jax.sharding import PartitionSpec as P

RT = 1.0 / 1331.0
L = 128
F32, BF16, I16, I32 = jnp.float32, jnp.bfloat16, jnp.int16, jnp.int32


def take(x, idx):
    dn = lax.GatherDimensionNumbers(offset_dims=(), collapsed_slice_dims=(1,), start_index_map=(1,),
                                    operand_batching_dims=(0,), start_indices_batching_dims=(0,))
    return lax.gather(x, idx[:, :, None], dn, (1, 1), mode=lax.GatherScatterMode.PROMISE_IN_BOUNDS)


def iota(shape, dim):
    return lax.broadcasted_iota(I32, shape, dim)


def to_cluster_rows(row, clusters):
    lane, sub = iota((8, L), 1), iota((8, L), 0)
    idx = 8 * (lane % 16) + sub
    part = lane // 16
    tiles = []
    for t in range((clusters + L - 1) // L):
        out = None
        for u in range(8):
            start = (8 * t + u) * L
            if start >= 8 * clusters:
                break
            got = take(row(start), idx)
            out = got if out is None else jnp.where(part == u, got, out)
        tiles.append(out)
    return tiles


def pair_kernel(count_ref, box_ref, lift_ref, halo_ref, pos_ref, par_ref, npos_ref, npar_ref, fpos_ref, fpar_ref,
                pl_ref, ex_ref, own_ref, near_ref, far_ref, vir_ref,
                tab_i, tab_j, jd, oh_j, oh_i, t_j, t_i, acc_j, acc_i, vacc):
    clusters = pos_ref.shape[1] // 8
    fars = halo_ref.shape[1]
    width = oh_j.shape[1]
    box = [box_ref[c] for c in range(3)]

    def row_of(pref, qref, c, lift):
        def row(start):
            if c < 3:
                r = pref[pl.ds(c, 1), pl.ds(start, L)]
                if c == 0 and lift is not None:
                    r = r + lift
            else:
                r = qref[pl.ds(c - 3, 1), pl.ds(start, L)]
            return jnp.broadcast_to(r, (8, L))
        return row

    tab_j[...] = jnp.zeros_like(tab_j)
    lane8 = iota((8, L), 1)
    for c in range(6):
        scale = (1.0, 1.0, 1.0, 1.0, 6.0, 12.0)[c]
        own = to_cluster_rows(row_of(pos_ref, par_ref, c, None), clusters)
        near = to_cluster_rows(row_of(npos_ref, npar_ref, c, lift_ref[0]), clusters)
        far = to_cluster_rows(row_of(fpos_ref, fpar_ref, c, lift_ref[1]), clusters)
        for t in range(2):
            tab_i[c, :, t * L:(t + 1) * L] = own[t] * scale if scale != 1.0 else own[t]
        half = clusters - L
        hal = jnp.broadcast_to(halo_ref[...], (8, fars))
        hal = jnp.concatenate([hal, jnp.zeros((8, L - fars), I32)], axis=1)
        fr = jnp.where(hal >= L, take(far[1], hal & (L - 1)), take(far[0], hal & (L - 1)))
        tab_j[c, :, 0:L] = own[0]
        rot0 = pltpu.roll(near[0], half, 1)
        rot1 = pltpu.roll(near[1], half, 1)
        tab_j[c, :, L:2 * L] = jnp.where(lane8 < half, own[1], rot0)
        tab_j[c, :, 2 * L:3 * L] = jnp.where(lane8 < half, rot0, rot1)
        tab_j[c, :, 3 * L:4 * L] = fr
    acc_j[...] = jnp.zeros_like(acc_j)
    acc_i[...] = jnp.zeros_like(acc_i)
    vacc[...] = jnp.zeros_like(vacc)

    sub = iota((8, L), 0)
    count = count_ref[0]
    shift0 = 8 * (sub % 2)
    bits = [jnp.left_shift(1, shift0 + ((sub + m) & 7)) for m in range(8)]
    base16 = iota((16, L), 0).astype(I16)
    one16 = jnp.ones((16, L), BF16)
    zero16 = jnp.zeros((16, L), BF16)

    def sub_chunk(g, first):
        cols = pl.ds(pl.multiple_of(first, L), L)
        here = slice(g * L, (g + 1) * L)
        ib = jnp.broadcast_to(pl_ref[pl.ds(0, 1), cols], (8, L))
        jb = jnp.broadcast_to(pl_ref[pl.ds(1, 1), cols], (8, L))
        sb = jnp.broadcast_to(pl_ref[pl.ds(2, 1), cols], (8, L))
        usable = lane8 < count - first
        w = [jnp.broadcast_to(ex_ref[pl.ds(k, 1), cols], (8, L)) for k in range(4)]
        words = jnp.where(sub < 4, jnp.where(sub < 2, w[0], w[1]), jnp.where(sub < 6, w[2], w[3]))
        words = jnp.where(usable, words, 0)
        il, ih = ib & (L - 1), ib >= L
        first_rows = [jnp.where(ih, take(tab_i[c, :, L:2 * L], il), take(tab_i[c, :, 0:L], il)) for c in range(6)]
        jl, jh, jm = jb & (L - 1), jb >= 2 * L, (jb & L) != 0
        second = []
        for c in range(6):
            q = [take(tab_j[c, :, t * L:(t + 1) * L], jl) for t in range(4)]
            second.append(jnp.where(jh, jnp.where(jm, q[3], q[2]), jnp.where(jm, q[1], q[0])))
        hi_y = jnp.where(sb >= 6, box[1], 0.0)
        lo_y = jnp.where(sb < 3, box[1], 0.0)
        s3 = sb - jnp.where(sb >= 6, 6, jnp.where(sb >= 3, 3, 0))
        hi_z = jnp.where(s3 == 2, box[2], 0.0)
        lo_z = jnp.where(s3 == 0, box[2], 0.0)
        xi, yi, zi, qi, ei, bi = first_rows
        yi, zi = yi - hi_y, zi - hi_z
        second[1] = second[1] - lo_y
        second[2] = second[2] - lo_z
        for c in range(6):
            jd[g, c, 0:8, :] = second[c]
            jd[g, c, 8:16, :] = second[c]
        fi, fj = [None] * 3, [None] * 3
        for m in range(7, -1, -1):
            xj, yj, zj, qj, ej, bj = [jd[g, c, m:m + 8, :] for c in range(6)] if m else second
            d = (xj - xi, yj - yi, zj - zi)
            r2 = d[0] * d[0] + d[1] * d[1] + d[2] * d[2]
            inv = lax.rsqrt(r2)
            inv2 = inv * inv
            inv6 = inv2 * inv2 * inv2
            s = qi * qj * (inv * inv2 - RT) + (bi * bj * inv6 - ei * ej) * (inv6 * inv2)
            s = jnp.where((words & bits[m]) != 0, s, 0.0)
            for c in range(3):
                f = s * d[c]
                fi[c] = f if fi[c] is None else fi[c] + f
                fj[c] = f if fj[c] is None else pltpu.roll(fj[c], 1, 0) + f
        origins = [jnp.broadcast_to(v[0:1, :], (8, L)) for v in (xi, yi, zi)]
        for c, v in enumerate((xi, yi, zi)):
            vacc[c] += fj[c] * (second[c] - origins[c]) - fi[c] * (v - origins[c])
        def split(fs):
            hi = [f.astype(BF16).astype(F32) for f in fs]
            lo = [f - h for f, h in zip(fs, hi)]
            return jnp.concatenate(hi + lo, axis=0).astype(BF16)
        tj = split(fj)
        j16 = jnp.broadcast_to(jb[0:1], (16, L)).astype(I16)
        i16 = jnp.broadcast_to(ib[0:1], (16, L)).astype(I16)
        upper = j16 >= 256
        for r in range(3):
            part = tj[16 * r:16 * r + 16]
            t_j[16 * r:16 * r + 16, here] = jnp.where(upper, zero16, part)
            t_j[48 + 16 * r:64 + 16 * r, here] = jnp.where(upper, part, zero16)
        t_i[:, here] = split(fi)
        j16 = j16 & 255
        for r in range(16):
            oh_j[16 * r:16 * r + 16, here] = jnp.where(base16 == j16 - 16 * r, one16, zero16)
        for r in range(clusters // 16):
            oh_i[16 * r:16 * r + 16, here] = jnp.where(base16 == i16 - 16 * r, one16, zero16)

    def step(b, carry):
        for g in range(width // L):
            sub_chunk(g, b * width + g * L)
        contract = (((1,), (1,)), ((), ()))
        acc_j[...] += lax.dot_general(t_j[...], oh_j[...], contract, preferred_element_type=F32)
        acc_i[...] += lax.dot_general(t_i[...], oh_i[...], contract, preferred_element_type=F32)
        return carry

    lax.fori_loop(0, (count + width - 1) // width, step, 0)

    fi = acc_i[0:24] + acc_i[24:48]
    fi = jnp.concatenate([fi, jnp.zeros((24, 2 * L - clusters), F32)], axis=1)
    lo_f = acc_j[0:24] + acc_j[24:48]
    hi_f = acc_j[48:72] + acc_j[72:96]
    tiles = [lo_f[:, 0:L], lo_f[:, L:], hi_f[:, 0:L], hi_f[:, L:]]
    hal = jnp.concatenate([halo_ref[...], jnp.full((1, L - fars), 4 * L, I32)], axis=1)
    oh_far = (jnp.broadcast_to(hal, (clusters, L)) == iota((clusters, L), 0)).astype(F32).astype(BF16)
    ff = tiles[3]
    f1 = ff.astype(BF16)
    r1 = ff - f1.astype(F32)
    f2 = r1.astype(BF16)
    f3 = (r1 - f2.astype(F32)).astype(BF16)
    far = sum(lax.dot_general(f, oh_far, (((1,), (1,)), ((), ())), preferred_element_type=F32) for f in (f3, f2, f1))
    far = jnp.concatenate([far, jnp.zeros((24, 2 * L - clusters), F32)], axis=1)
    far = [far[:, 0:L], far[:, L:]]
    pick = sub == (lane8 & 7)

    def atom_order(src, base, c, t, ref, minus=None):
        slot = base + 16 * t
        idx = (slot % L) + lane8 // 8
        got = take(src[slot // L][8 * c:8 * c + 8], idx)
        if minus is not None:
            got = got - take(minus[(16 * t) // L][8 * c:8 * c + 8], (16 * t) % L + lane8 // 8)
        ref[c:c + 1, t * L:(t + 1) * L] = jnp.sum(jnp.where(pick, got, 0.0), axis=0, keepdims=True)

    mi = [fi[:, 0:L], fi[:, L:]]
    for c in range(3):
        for t in range(clusters // 16):
            atom_order(tiles, 0, c, t, own_ref, mi)
            atom_order(tiles, clusters, c, t, near_ref)
            atom_order(far, 0, c, t, far_ref)
    for c in range(3):
        vir_ref[c:c + 1, :] = jnp.sum(vacc[c], axis=0, keepdims=True)


def pair_forces(count, box, lifts, halo, pos, par, npos, npar, fpos, fpar, pairs, words, width=512):
    smem = pl.BlockSpec(memory_space=pltpu.SMEM)
    vmem = pl.BlockSpec(memory_space=pltpu.VMEM)
    atoms = pos.shape[1]
    clusters = atoms // 8
    out = jax.ShapeDtypeStruct((3, atoms), F32)
    return pl.pallas_call(
        pair_kernel,
        out_shape=(out, out, out, jax.ShapeDtypeStruct((3, L), F32)),
        in_specs=[smem] * 3 + [vmem] * 9,
        out_specs=(vmem,) * 4,
        scratch_shapes=[
            pltpu.VMEM((6, 8, 2 * L), F32),
            pltpu.VMEM((6, 8, 4 * L), F32),
            pltpu.VMEM((width // L, 6, 16, L), F32),
            pltpu.VMEM((256, width), BF16),
            pltpu.VMEM((clusters, width), BF16),
            pltpu.VMEM((96, width), BF16),
            pltpu.VMEM((48, width), BF16),
            pltpu.VMEM((96, 256), F32),
            pltpu.VMEM((48, clusters), F32),
            pltpu.VMEM((3, 8, L), F32),
        ],
        name="pair_forces",
    )(count, box, lifts, halo, pos, par, npos, npar, fpos, fpar, pairs, words)


time_step = 0.25
thermal_scale_unit = 2.0
reservoir_inertia_mass = 4.0
barostat_gain = 0.1
pressure_target = 1.0


def passed_along(value, axis, steps):
    count = lax.axis_size(axis)
    pairs = [(source, (source + steps) % count) for source in range(count)]
    return lax.ppermute(value, axis, pairs)


def on_device(
    positions,
    velocities,
    atom_params,
    pair_list,
    pair_count,
    exclusion,
    halo_far,
    box_lengths,
    extended_variables,
):
    atoms_here = positions.shape[1]
    index, count = lax.axis_index("gx"), lax.axis_size("gx")
    inverse_mass = atom_params[3]
    kinetic = 0.5 * jnp.sum(velocities * velocities / inverse_mass[None, :], axis=1)
    packed = jnp.concatenate([positions, atom_params], axis=0)
    near_in = passed_along(packed, "gx", -1)
    far_in = passed_along(packed, "gx", -2)
    halo_in = passed_along(halo_far, "gx", -2)
    lifts = jnp.where(jnp.stack([index + 1, index + 2]) >= count, box_lengths[0], 0.0)
    own, near, far, virial = pair_forces(
        pair_count, box_lengths, lifts, halo_in[None], positions, atom_params,
        near_in[:3], near_in[3:], far_in[:3], far_in[3:], pair_list, exclusion,
    )
    virial = -0.5 * jnp.sum(virial, axis=1)
    forces = own + passed_along(near, "gx", 1) + passed_along(far, "gx", 2)
    sums = lax.psum(jnp.stack([kinetic, virial]), "gx")
    kinetic, virial = sums[0], sums[1]
    total = jnp.sum(kinetic)
    volume = box_lengths[0] * box_lengths[1] * box_lengths[2]
    ratio = 2.0 * total / (3.0 * (atoms_here * count) * thermal_scale_unit)
    damping = extended_variables[0] + reservoir_inertia_mass * (ratio - 1.0)
    box_rates = extended_variables[1:] + barostat_gain * (
        kinetic - virial - pressure_target * volume / 2.0
    ) / (total / 3.0)
    new_velocities = velocities + time_step * (
        forces * inverse_mass[None, :] - (damping + box_rates[:, None]) * velocities
    )
    new_positions = positions * (1.0 + time_step * box_rates[:, None]) + time_step * new_velocities
    return forces, new_velocities, new_positions, jnp.concatenate([damping[None], box_rates])


def solution(mesh):
    whole = ("rep", "gx")
    rows, flat = P(None, whole), P(whole)
    return jax.shard_map(
        on_device,
        mesh=mesh,
        in_specs=(rows, rows, rows, rows, flat, rows, flat, P("rep"), P("rep")),
        out_specs=(rows, rows, rows, P("rep")),
        check_vma=False,
    )
```

time: 500 us -> 307 us (0.61)
  local copies, waits for them, and re-layouts: 135 us -> 4.41 us
  other arithmetic: 66.6 us -> 5 us
  matrix products: 15 us -> 0 us
  blocking collectives: 240 us -> 251 us
  Pallas kernels: 0 us -> 9.92 us
    slice x92 -> x4, local copies, waits for them, and re-layouts: 85.9 us -> 2.46 us  [the longest x1 0.62 us: on_device(): far_in[3:]]
    gather x14 -> x0, local copies, waits for them, and re-layouts: 33.1 us -> none  [the longest x6 16.2 us: pair_tiles(): jnp.take(slot_table, pair_rows[0], axis=0).T.reshape(6, 8, tile_width)]
    dot_general x6 -> x0, matrix products: 15 us -> none  [one_block(): jnp.dot(selector, tile_terms, precision=lax.Precision.HIGHEST, preferred_...]
    add x10 -> x1, other arithmetic: 12.6 us -> 0.01 us  [on_device(): damping + box_rates[:, None]]
    psum x3 -> x1, blocking collectives: 240 us -> 251 us  [on_device(): sums = lax.psum(jnp.stack([kinetic, virial]), 'gx')]
    pallas_call x0 -> x1, Pallas kernels: none -> 9.92 us  [pair_forces(): pl.pallas_call(pair_kernel, out_shape=(out, out, out, jax.ShapeDtypeStruc...]
    mul x7 -> x1, other arithmetic: 8.59 us -> 0.01 us  [on_device(): virial = -0.5 * jnp.sum(virial, axis=1)]
    lt x6 -> x0, other arithmetic: 7.47 us -> none  [one_block(): usable = first_row + jnp.arange(block_rows, dtype=jnp.int32) < pair_total]
  transfers between devices with their start and end apart: 4 -> 5, of which waited for: 2 -> 2; matrix products, arithmetic and copies ran while one was open for 1% -> 2% of each run, Pallas kernels for 0% -> 0%
where the time goes in v1:
time: 307 us
  blocking collectives  251 us (82%)
  starting transfers between devices  26.2 us (9%)
  Pallas kernels  9.92 us (3%)
  waiting for transfers between devices  6.61 us (2%)
  other arithmetic  5 us (2%)
  between operations  4.65 us (2%)
  local copies, waits for them, and re-layouts  4.41 us (1%)
    psum x1, blocking collectives, on_device(): sums = lax.psum(jnp.stack([kinetic, virial]), 'gx')  251 us
    ppermute x5, starting transfers between devices, passed_along(): return lax.ppermute(value, axis, pairs)  26.2 us
    pallas_call x1, Pallas kernels, pair_forces(): pl.pallas_call(pair_kernel, out_shape=(out, out, out, jax.ShapeDtypeStruc...  9.92 us
    ppermute x5, waiting for transfers between devices, passed_along(): return lax.ppermute(value, axis, pairs)  6.61 us
  transfers between devices with their start and end apart: 5, of which 2 were waited for; matrix products, arithmetic and copies ran while one was open for 2% of the time, Pallas kernels for 0%

profile of v1, /device:TPU:40, one launch (start us, length us, event | category | flops | bytes accessed | tf_op | source)
XLA Modules:
  0.0 307.5 jit_solution(15925441781769985983)
XLA Ops:
  0.6 0.0 copy-start.3
  0.7 0.8 pad_maximum_fusion
  1.4 0.0 copy-start.1
  1.4 24.6 %collective-permute-start.1 = (f32[7,1536]{1,0:T(8,128)S(1)}, f32[7,1536]{1,0:T(8,128)S(1)}, u32[]{:S(2)}, u32[]{:S(2)}) collective-permute-start(f32[7,1536]{1,0:T(8,128)S(1)} %pad_maximum_fusion), channel_id=1, source_target_pairs={{0,127},{1,0},{2,1},{3,2},{4,3},{5,4},{6,5},{7,6},{8,7},{9,8},{10,... | collective-permute-start | bytes 129032 | tf_op jit(solution)/shard_map/ppermute | solution.py:239
  26.0 0.7 collective-permute-start.2
  26.7 0.0 copy-done.6
  26.7 0.6 collective-permute-start
  27.4 0.8 slice_reduce_fusion
  28.1 0.0 copy-done.3
  28.1 0.7 fusion.1
  28.8 0.1 fusion
  28.9 1.3 compare_select_fusion.lift_ref
  32.8 0.0 collective-permute-done.1
  32.8 0.6 slice.49.npos_ref
  33.4 0.6 slice.50.npar_ref
  34.0 0.0 collective-permute-done.2
  34.0 0.6 slice.51.fpos_ref
  34.7 0.6 slice.52.fpar_ref
  35.3 0.0 collective-permute-done
  35.3 0.5 copy-done.5
  35.8 9.9 %pair_forces.1 = (f32[3,1536]{1,0:T(4,128)}, f32[3,1536]{1,0:T(4,128)}, f32[3,1536]{1,0:T(4,128)}, f32[3,128]{1,0:T(4,128)}) custom-call(s32[1]{0:T(128)S(6)} %copy.13.count_ref, f32[3]{0:T(128)} %box_ref.1, f32[2]{0:T(128)} %compare_select_fusion.lift_ref, s32[1,96]{1,0:T(1,128)} %bitcast.17, f32[3,1536]{1,0:T(4,128)} %pos_ref.1, f32[4,1536]{1,0:T(4,128)} %par_ref.1, ...), custom_call_target="tpu_custom_call" | custom-call | tf_op jit(solution)/shard_map/pair_forces/pallas_call | solution.py:208
  45.7 0.8 reduce_sum.28
  46.6 250.7 %psum.7 = f32[2,3]{1,0:T(2,128)S(1)} all-reduce(f32[2,3]{1,0:T(2,128)S(1)} %pad_maximum_fusion.1), channel_id=1, replica_groups=mesh['rep'=2,'gx'=128] {'gx'}, use_global_device_ids=true, to_apply=%region_2.3 | all-reduce | flops 6 | bytes 48 | tf_op jit(solution)/shard_map/psum | solution.py:268
  297.3 0.6 slice_reduce_fusion.1
  299.2 0.1 collective-permute-start.3
  299.3 0.1 collective-permute-start.4
  299.4 0.0 copy-done.4
  299.5 0.1 multiply_add_fusion.2
  299.6 0.6 pad_maximum_fusion.2
  300.2 5.9 %collective-permute-done.3 = f32[3,1536]{1,0:T(4,128)S(1)} collective-permute-done((f32[3,1536]{1,0:T(4,128)}, f32[3,1536]{1,0:T(4,128)S(1)}, u32[]{:S(2)}, u32[]{:S(2)}) %collective-permute-start.3) | collective-permute-done | bytes 18464 | tf_op jit(solution)/shard_map/ppermute | solution.py:239
  306.1 0.7 collective-permute-done.4
  306.8 0.7 multiply_add_fusion
  (11 shorter events, 0.0 us)
Async XLA Ops:
  0.6 26.1 %copy-start.6 = (s32[96]{0:T(128)S(1)}, s32[96]{0:T(128)}, u32[]{:S(2)}) copy-start(s32[96]{0:T(128)} %param.15) | copy-start | bytes 1156
  0.6 27.5 %copy-start.3 = (f32[3]{0:T(128)S(1)}, f32[3]{0:T(128)}, u32[]{:S(2)}) copy-start(f32[3]{0:T(128)} %box_ref.1) | copy-start | bytes 40
  1.4 27.4 %copy-start.1 = (f32[3,1536]{1,0:T(4,128)S(1)}, f32[3,1536]{1,0:T(4,128)}, u32[]{:S(2)}) copy-start(f32[3,1536]{1,0:T(4,128)} %param.10) | copy-start | bytes 55300
  1.4 31.4 %collective-permute-start.1 = (f32[7,1536]{1,0:T(8,128)S(1)}, f32[7,1536]{1,0:T(8,128)S(1)}, u32[]{:S(2)}, u32[]{:S(2)}) collective-permute-start(f32[7,1536]{1,0:T(8,128)S(1)} %pad_maximum_fusion), channel_id=1, source_target_pairs={{0,127},{1,0},{2,1},{3,2},{4,3},{5,4},{6,5},{7,6},{8,7},{9,8},{10,... | collective-permute-start | bytes 129032 | tf_op jit(solution)/shard_map/ppermute | solution.py:239
  26.0 8.0 %collective-permute-start.2 = (f32[7,1536]{1,0:T(8,128)S(1)}, f32[7,1536]{1,0:T(8,128)S(1)}, u32[]{:S(2)}, u32[]{:S(2)}) collective-permute-start(f32[7,1536]{1,0:T(8,128)S(1)} %pad_maximum_fusion), channel_id=1, source_target_pairs={{0,126},{1,127},{2,0},{3,1},{4,2},{5,3},{6,4},{7,5},{8,6},{9,7},{1... | collective-permute-start | bytes 129032 | tf_op jit(solution)/shard_map/ppermute | solution.py:239
  26.7 8.5 %collective-permute-start = (s32[96]{0:T(128)S(1)}, s32[96]{0:T(128)S(1)}, u32[]{:S(2)}, u32[]{:S(2)}) collective-permute-start(s32[96]{0:T(128)S(1)} %copy-done.6), channel_id=1, source_target_pairs={{0,126},{1,127},{2,0},{3,1},{4,2},{5,3},{6,4},{7,5},{8,6},{9,7},{1... | collective-permute-start | bytes 1160 | tf_op jit(solution)/shard_map/ppermute | solution.py:239
  35.3 0.5 copy-start.5
  35.8 263.7 %copy-start.4 = (f32[4]{0:T(128)S(1)}, f32[4]{0:T(128)}, u32[]{:S(2)}) copy-start(f32[4]{0:T(128)} %param.17) | copy-start | bytes 52
  45.7 261.1 %copy-start = (f32[3,1536]{1,0:T(4,128)S(1)}, f32[3,1536]{1,0:T(4,128)}, u32[]{:S(2)}) copy-start(f32[3,1536]{1,0:T(4,128)} %pos_ref.1) | copy-start | bytes 55300
  45.7 261.1 %copy-start.2 = (f32[3,1536]{1,0:T(4,128)S(1)}, f32[3,1536]{1,0:T(4,128)}, u32[]{:S(2)}) copy-start(f32[3,1536]{1,0:T(4,128)} %get-tuple-element.8) | copy-start | bytes 55300
  299.2 6.9 %collective-permute-start.3 = (f32[3,1536]{1,0:T(4,128)}, f32[3,1536]{1,0:T(4,128)S(1)}, u32[]{:S(2)}, u32[]{:S(2)}) collective-permute-start(f32[3,1536]{1,0:T(4,128)} %get-tuple-element.9), channel_id=1, source_target_pairs={{0,1},{1,2},{2,3},{3,4},{4,5},{5,6},{6,7},{7,8},{8,9},{9,10},{10,1... | collective-permute-start | bytes 55304 | tf_op jit(solution)/shard_map/ppermute | solution.py:239
  299.3 7.5 %collective-permute-start.4 = (f32[3,1536]{1,0:T(4,128)}, f32[3,1536]{1,0:T(4,128)S(1)}, u32[]{:S(2)}, u32[]{:S(2)}) collective-permute-start(f32[3,1536]{1,0:T(4,128)} %get-tuple-element.10), channel_id=1, source_target_pairs={{0,2},{1,3},{2,4},{3,5},{4,6},{5,7},{6,8},{7,9},{8,10},{9,11},{10,... | collective-permute-start | bytes 55304 | tf_op jit(solution)/shard_map/ppermute | solution.py:239

commit v2 on v1

v2 whole, which is shorter than its diff:
```python
import functools

import jax
import jax.numpy as jnp
from jax import lax
from jax.experimental import pallas as pl
from jax.experimental.pallas import tpu as pltpu
from jax.sharding import PartitionSpec as P

PLANE = 8
WIDTH = 512
MESH = pl.DeviceIdType.MESH

time_step = 0.25
thermal_scale_unit = 2.0
reservoir_inertia_mass = 4.0
barostat_gain = 0.1
pressure_target = 1.0

RT = 1.0 / 1331.0
L = 128
F32, BF16, I16, I32 = jnp.float32, jnp.bfloat16, jnp.int16, jnp.int32


def take(x, idx):
    dn = lax.GatherDimensionNumbers(offset_dims=(), collapsed_slice_dims=(1,), start_index_map=(1,),
                                    operand_batching_dims=(0,), start_indices_batching_dims=(0,))
    return lax.gather(x, idx[:, :, None], dn, (1, 1), mode=lax.GatherScatterMode.PROMISE_IN_BOUNDS)


def iota(shape, dim):
    return lax.broadcasted_iota(I32, shape, dim)


def to_cluster_rows(row, clusters):
    lane, sub = iota((8, L), 1), iota((8, L), 0)
    idx = 8 * (lane % 16) + sub
    part = lane // 16
    tiles = []
    for t in range((clusters + L - 1) // L):
        out = None
        for u in range(8):
            start = (8 * t + u) * L
            if start >= 8 * clusters:
                break
            got = take(row(start), idx)
            out = got if out is None else jnp.where(part == u, got, out)
        tiles.append(out)
    return tiles


def step_kernel(
    domains, count_ref, box_ref, ext_ref, halo_ref, pos_ref, vel_ref, par_ref, pl_ref, ex_ref,
    force_ref, nvel_ref, npos_out, coup_ref,
    npos_ref, npar_ref, fpos_ref, fpar_ref, fhalo_ref, near_ref, far_ref, near_in, far_in,
    part, src1, src2, sum1, sum2,
    tab_i, tab_j, jd, ri, wd, fs, acc_j, acc_i, vacc,
    halo_send, halo_recv, force_send, force_recv, send1, recv1, send2, recv2,
):
    planes = domains // PLANE
    me = lax.axis_index("gx")
    place, plane = lax.rem(me, PLANE), lax.div(me, PLANE)
    at = lambda shift: lax.rem(me + domains + shift, domains)
    mates = [plane * PLANE + lax.rem(place + k, PLANE) for k in range(1, PLANE)]
    columns = [lax.rem(plane + k, planes) * PLANE + place for k in range(1, planes)]

    barrier = pltpu.get_barrier_semaphore()
    greeted = [at(-1), at(-2), at(1), at(2)] + mates + columns
    for other in greeted:
        pl.semaphore_signal(barrier, inc=1, device_id={"gx": other}, device_id_type=MESH)

    def copy(src, dst, send, recv, other):
        return pltpu.make_async_remote_copy(
            src_ref=src, dst_ref=dst, send_sem=send, recv_sem=recv, device_id={"gx": other}, device_id_type=MESH
        )

    halo_copies = [
        copy(pos_ref, npos_ref, halo_send.at[0], halo_recv.at[0], at(-1)),
        copy(par_ref, npar_ref, halo_send.at[1], halo_recv.at[1], at(-1)),
        copy(pos_ref, fpos_ref, halo_send.at[2], halo_recv.at[2], at(-2)),
        copy(par_ref, fpar_ref, halo_send.at[3], halo_recv.at[3], at(-2)),
        copy(halo_ref, fhalo_ref, halo_send.at[4], halo_recv.at[4], at(-2)),
    ]
    clusters = pos_ref.shape[1] // 8
    fars = fhalo_ref.shape[1]
    width = fs.shape[0] * L
    box = [box_ref[c] for c in range(3)]

    def row_of(pref, qref, c, lift):
        def row(start):
            if c < 3:
                r = pref[pl.ds(c, 1), pl.ds(start, L)]
                if c == 0 and lift is not None:
                    r = r + lift
            else:
                r = qref[pl.ds(c - 3, 1), pl.ds(start, L)]
            return jnp.broadcast_to(r, (8, L))
        return row

    lane8 = iota((8, L), 1)
    tiles_of = clusters // 16
    half = clusters - L
    scales = (1.0, 1.0, 1.0, 1.0, 6.0, 12.0)
    for c in range(6):
        own = to_cluster_rows(row_of(pos_ref, par_ref, c, None), clusters)
        for t in range(2):
            tab_i[c, :, t * L:(t + 1) * L] = own[t] * scales[c] if scales[c] != 1.0 else own[t]
            tab_j[c, :, t * L:(t + 1) * L] = own[t]
    part[...] = jnp.zeros_like(part)
    kin = None
    for t in range(tiles_of):
        cols = slice(t * L, (t + 1) * L)
        term = vel_ref[:, cols] * vel_ref[:, cols] / par_ref[3:4, cols]
        kin = term if kin is None else kin + term
    part[0:3, :] = 0.5 * kin
    acc_j[...] = jnp.zeros_like(acc_j)
    acc_i[...] = jnp.zeros_like(acc_i)
    vacc[...] = jnp.zeros_like(vacc)
    fs[...] = jnp.zeros_like(fs)

    pl.semaphore_wait(barrier, len(greeted))
    for item in halo_copies:
        item.start()
    for item in halo_copies:
        item.wait()

    lift_near = jnp.where(me + 1 >= domains, box[0], 0.0)
    lift_far = jnp.where(me + 2 >= domains, box[0], 0.0)
    hal = jnp.concatenate(
        [jnp.broadcast_to(fhalo_ref[...], (8, fars)), jnp.zeros((8, L - fars), I32)], axis=1)
    for c in range(6):
        near = to_cluster_rows(row_of(npos_ref, npar_ref, c, lift_near), clusters)
        far = to_cluster_rows(row_of(fpos_ref, fpar_ref, c, lift_far), clusters)
        rot0 = pltpu.roll(near[0], half, 1)
        rot1 = pltpu.roll(near[1], half, 1)
        tab_j[c, :, L:2 * L] = jnp.where(lane8 < half, tab_j[c, :, L:2 * L], rot0)
        tab_j[c, :, 2 * L:3 * L] = jnp.where(lane8 < half, rot0, rot1)
        tab_j[c, :, 3 * L:4 * L] = jnp.where(
            hal >= L, take(far[1], hal & (L - 1)), take(far[0], hal & (L - 1)))


    sub = iota((8, L), 0)
    count = count_ref[0]
    shift0 = 8 * (sub % 2)
    bits = [jnp.left_shift(1, shift0 + ((sub + m) & 7)) for m in range(8)]
    one16 = jnp.ones((16, L), BF16)
    zero16 = jnp.zeros((16, L), BF16)

    groups = width // L
    base16 = iota((16, L), 0).astype(I16)

    def gather(block):
        for g in range(groups):
            first = block * width + g * L
            cols = pl.ds(pl.multiple_of(first, L), L)
            ib = jnp.broadcast_to(pl_ref[pl.ds(0, 1), cols], (8, L))
            jb = jnp.broadcast_to(pl_ref[pl.ds(1, 1), cols], (8, L))
            sb = jnp.broadcast_to(pl_ref[pl.ds(2, 1), cols], (8, L))
            usable = lane8 < count - first
            w = [jnp.broadcast_to(ex_ref[pl.ds(k, 1), cols], (8, L)) for k in range(4)]
            words = jnp.where(sub < 4, jnp.where(sub < 2, w[0], w[1]), jnp.where(sub < 6, w[2], w[3]))
            wd[g] = jnp.where(usable, words, 0)
            above_y, below_y = sb >= 6, sb < 3
            s3 = sb - jnp.where(above_y, 6, jnp.where(below_y, 0, 3))
            il, ih = ib & (L - 1), ib >= L
            jl, jh, jm = jb & (L - 1), jb >= 2 * L, (jb & L) != 0
            for c in range(6):
                v = jnp.where(ih, take(tab_i[c, :, L:2 * L], il), take(tab_i[c, :, 0:L], il))
                if c in (1, 2):
                    v = v - jnp.where(above_y if c == 1 else s3 == 2, box[c], 0.0)
                ri[g, c] = v
            for c in range(6):
                q = [take(tab_j[c, :, t * L:(t + 1) * L], jl) for t in range(4)]
                v = jnp.where(jh, jnp.where(jm, q[3], q[2]), jnp.where(jm, q[1], q[0]))
                if c in (1, 2):
                    v = v - jnp.where(below_y if c == 1 else s3 == 0, box[c], 0.0)
                jd[g, c, 0:8, :] = v
                jd[g, c, 8:16, :] = v

    def split(fs):
        hi = [f.astype(BF16).astype(F32) for f in fs]
        lo = [f - h for f, h in zip(fs, hi)]
        return jnp.concatenate(hi + lo, axis=0).astype(BF16)

    def compute(block):
        for g in range(groups):
            xi, yi, zi, qi, ei, bi = [ri[g, c] for c in range(6)]
            words = wd[g]
            fi, fj = [None] * 3, [None] * 3
            for m in range(7, -1, -1):
                xj, yj, zj, qj, ej, bj = [jd[g, c, m:m + 8, :] for c in range(6)]
                d = (xj - xi, yj - yi, zj - zi)
                r2 = d[0] * d[0] + d[1] * d[1] + d[2] * d[2]
                inv = lax.rsqrt(r2)
                inv2 = inv * inv
                inv3 = inv * inv2
                inv6 = inv3 * inv3
                s = qi * qj * (inv3 - RT) + (bi * bj * inv6 - ei * ej) * (inv6 * inv2)
                s = jnp.where((words & bits[m]) != 0, s, 0.0)
                for c in range(3):
                    f = s * d[c]
                    fi[c] = f if fi[c] is None else fi[c] + f
                    fj[c] = f if fj[c] is None else pltpu.roll(fj[c], 1, 0) + f
            for c, v in enumerate((xi, yi, zi)):
                origin = jnp.broadcast_to(ri[g, c, 0:1, :], (8, L))
                vacc[c] += fj[c] * (jd[g, c, 0:8, :] - origin) - fi[c] * (v - origin)
            for c in range(3):
                fs[g, c] = fj[c]
                fs[g, 3 + c] = fi[c]

    half_c = clusters // 2

    def dots(block):
        tjs, tis, ojs, ois = [], [], [], []
        for g in range(groups):
            cols = pl.ds(pl.multiple_of(block * width + g * L, L), L)
            j16 = jnp.broadcast_to(pl_ref[pl.ds(1, 1), cols], (16, L)).astype(I16)
            i16 = jnp.broadcast_to(pl_ref[pl.ds(0, 1), cols], (16, L)).astype(I16)
            tj = split([fs[g, c] for c in range(3)])
            ti = split([fs[g, 3 + c] for c in range(3)])
            parts = lambda t: [t[16 * r:16 * r + 16] for r in range(3)]
            which = j16 & (3 * L)
            tjs.append(jnp.concatenate(
                [jnp.where(which == k * L, p, zero16) for k in range(4) for p in parts(tj)], axis=0))
            later = i16 >= half_c
            tis.append(jnp.concatenate(
                [jnp.where(later, zero16, p) for p in parts(ti)] + [jnp.where(later, p, zero16) for p in parts(ti)], axis=0))
            j16 = j16 & (L - 1)
            i16 = jnp.where(later, i16 - half_c, i16)
            ojs.append(jnp.concatenate([jnp.where(base16 == j16 - 16 * r, one16, zero16) for r in range(L // 16)], axis=0))
            ois.append(jnp.concatenate([jnp.where(base16 == i16 - 16 * r, one16, zero16) for r in range(half_c // 16)], axis=0))
        contract = (((1,), (1,)), ((), ()))
        wide = lambda xs: jnp.concatenate(xs, axis=1)
        acc_j[...] += lax.dot_general(wide(tjs), wide(ojs), contract, preferred_element_type=F32)
        acc_i[...] += lax.dot_general(wide(tis), wide(ois), contract, preferred_element_type=F32)

    blocks = pl_ref.shape[1] // width

    def step(block, carry):
        dots(jnp.maximum(block - 1, 0))
        compute(block)
        gather(jnp.minimum(block + 1, blocks - 1))
        return carry

    gather(0)
    lax.fori_loop(0, blocks, step, 0)
    dots(blocks - 1)

    pad = jnp.zeros((24, L - half_c), F32)
    mi = [acc_i[48 * k:48 * k + 24] + acc_i[48 * k + 24:48 * k + 48] for k in range(2)]
    mi = [jnp.concatenate([v, pad], axis=1) for v in mi]
    tiles = [acc_j[48 * k:48 * k + 24] + acc_j[48 * k + 24:48 * k + 48] for k in range(4)]
    hal = jnp.concatenate([fhalo_ref[...], jnp.full((1, L - fars), 4 * L, I32)], axis=1)
    oh_far = (jnp.broadcast_to(hal, (clusters, L)) == iota((clusters, L), 0)).astype(F32).astype(BF16)
    ff = tiles[3]
    f1 = ff.astype(BF16)
    r1 = ff - f1.astype(F32)
    f2 = r1.astype(BF16)
    f3 = (r1 - f2.astype(F32)).astype(BF16)
    far = sum(lax.dot_general(f, oh_far, (((1,), (1,)), ((), ())), preferred_element_type=F32) for f in (f3, f2, f1))
    far = jnp.concatenate([far, jnp.zeros((24, 2 * L - clusters), F32)], axis=1)
    far = [far[:, 0:L], far[:, L:]]
    pick = sub == (lane8 & 7)

    def atom_order(src, base, c, t, ref, minus=None):
        slot = base + 16 * t
        idx = (slot % L) + lane8 // 8
        got = take(src[slot // L][8 * c:8 * c + 8], idx)
        if minus is not None:
            mine = minus[(16 * t) // half_c][8 * c:8 * c + 8]
            got = got - take(mine, (16 * t) % half_c + lane8 // 8)
        ref[c:c + 1, t * L:(t + 1) * L] = jnp.sum(jnp.where(pick, got, 0.0), axis=0, keepdims=True)

    for c in range(3):
        part[3 + c:4 + c, :] = -0.5 * jnp.sum(vacc[c], axis=0, keepdims=True)
    sums = jnp.sum(part[...], axis=1, keepdims=True)
    row = jnp.sum(jnp.where(sub == lane8, jnp.broadcast_to(sums, (8, L)), 0.0), axis=0, keepdims=True)
    src1[...] = row
    sum1[place] = src1[...]
    for c in range(3):
        for t in range(tiles_of):
            atom_order(tiles, clusters, c, t, near_ref)
    plane_copies = [
        copy(src1, sum1.at[place], send1.at[k], recv1.at[place], mate) for k, mate in enumerate(mates)]
    for item in plane_copies:
        item.start()
    for c in range(3):
        for t in range(tiles_of):
            atom_order(far, 0, c, t, far_ref)
    near_copy = copy(near_ref, near_in, force_send.at[0], force_recv.at[0], at(1))
    near_copy.start()
    for c in range(3):
        for t in range(tiles_of):
            atom_order(tiles, 0, c, t, force_ref, mi)
    far_copy = copy(far_ref, far_in, force_send.at[1], force_recv.at[1], at(2))
    far_copy.start()
    for k in range(1, PLANE):
        other = lax.rem(place + k, PLANE)
        copy(src1, sum1.at[other], send1.at[k - 1], recv1.at[other], mates[k - 1]).wait_recv()
    row = sum1[0]
    for k in range(1, PLANE):
        row = row + sum1[k]
    src2[...] = row
    sum2[plane] = src2[...]
    column_copies = [
        copy(src2, sum2.at[plane], send2.at[k], recv2.at[plane], other) for k, other in enumerate(columns)]
    for item in column_copies:
        item.start()
    near_copy.wait()
    far_copy.wait()
    force_ref[...] = force_ref[...] + near_in[...] + far_in[...]
    for item in plane_copies:
        item.wait_send()
    for k in range(1, planes):
        other = lax.rem(plane + k, planes)
        copy(src2, sum2.at[other], send2.at[k - 1], recv2.at[other], columns[k - 1]).wait_recv()
    row = sum2[0]
    for k in range(1, planes):
        row = row + sum2[k]
    row = jnp.broadcast_to(row, (8, L))
    one_of = [take(row, jnp.full((8, L), c, I32)) for c in range(6)]
    total = one_of[0] + one_of[1] + one_of[2]
    volume = box[0] * box[1] * box[2]
    ratio = 2.0 * total / (3.0 * (8 * clusters * domains) * thermal_scale_unit)
    damping = ext_ref[0] + reservoir_inertia_mass * (ratio - 1.0)
    coup_ref[0] = damping[0, 0]
    for c in range(3):
        rate = ext_ref[1 + c] + barostat_gain * (
            one_of[c] - one_of[3 + c] - pressure_target * volume / 2.0
        ) / (total / 3.0)
        coup_ref[1 + c] = rate[0, 0]
        drag, grow = (damping + rate)[0:1], (1.0 + time_step * rate)[0:1]
        for t in range(tiles_of):
            cols = slice(t * L, (t + 1) * L)
            v = vel_ref[c:c + 1, cols]
            v = v + time_step * (force_ref[c:c + 1, cols] * par_ref[3:4, cols] - drag * v)
            nvel_ref[c:c + 1, cols] = v
            npos_out[c:c + 1, cols] = pos_ref[c:c + 1, cols] * grow + time_step * v
    for item in column_copies:
        item.wait_send()


def on_device(
    positions,
    velocities,
    atom_params,
    pair_list,
    pair_count,
    exclusion,
    halo_far,
    box_lengths,
    extended_variables,
):
    domains = lax.axis_size("gx")
    planes = domains // PLANE
    atoms, fars = positions.shape[1], halo_far.shape[0]
    clusters, groups = atoms // 8, WIDTH // L
    smem = pl.BlockSpec(memory_space=pltpu.SMEM)
    vmem = pl.BlockSpec(memory_space=pltpu.VMEM)
    rows = jax.ShapeDtypeStruct((3, atoms), F32)
    dma = pltpu.SemaphoreType.DMA
    return pl.pallas_call(
        functools.partial(step_kernel, domains),
        out_shape=(rows, rows, rows, jax.ShapeDtypeStruct((4,), F32)),
        in_specs=[smem] * 3 + [vmem] * 6,
        out_specs=(vmem, vmem, vmem, smem),
        scratch_shapes=[
            pltpu.VMEM((3, atoms), F32),
            pltpu.VMEM((4, atoms), F32),
            pltpu.VMEM((3, atoms), F32),
            pltpu.VMEM((4, atoms), F32),
            pltpu.VMEM((1, fars), I32),
            pltpu.VMEM((3, atoms), F32),
            pltpu.VMEM((3, atoms), F32),
            pltpu.VMEM((3, atoms), F32),
            pltpu.VMEM((3, atoms), F32),
            pltpu.VMEM((8, L), F32),
            pltpu.VMEM((1, L), F32),
            pltpu.VMEM((1, L), F32),
            pltpu.VMEM((PLANE, 1, L), F32),
            pltpu.VMEM((planes, 1, L), F32),
            pltpu.VMEM((6, 8, 2 * L), F32),
            pltpu.VMEM((6, 8, 4 * L), F32),
            pltpu.VMEM((groups, 6, 16, L), F32),
            pltpu.VMEM((groups, 6, 8, L), F32),
            pltpu.VMEM((groups, 8, L), I32),
            pltpu.VMEM((groups, 6, 8, L), F32),
            pltpu.VMEM((192, L), F32),
            pltpu.VMEM((96, clusters // 2), F32),
            pltpu.VMEM((3, 8, L), F32),
            dma((5,)),
            dma((5,)),
            dma((2,)),
            dma((2,)),
            dma((PLANE - 1,)),
            dma((PLANE,)),
            dma((planes - 1,)),
            dma((planes,)),
        ],
        compiler_params=pltpu.CompilerParams(collective_id=0, has_side_effects=True),
        name="force_step",
    )(pair_count, box_lengths, extended_variables, halo_far[None], positions, velocities, atom_params,
      pair_list, exclusion)


def solution(mesh):
    whole = ("rep", "gx")
    rows, flat = P(None, whole), P(whole)
    return jax.shard_map(
        on_device,
        mesh=mesh,
        in_specs=(rows, rows, rows, rows, flat, rows, flat, P("rep"), P("rep")),
        out_specs=(rows, rows, rows, P("rep")),
        check_vma=False,
    )
```

time: 307 us -> 59.9 us (0.20)
  blocking collectives: 251 us -> 0 us
  Pallas kernels: 9.92 us -> 54.9 us
  starting transfers between devices: 26.2 us -> 0 us
  waiting for transfers between devices: 6.61 us -> 0 us
  other arithmetic: 5 us -> 0 us
  between operations: 4.65 us -> 1.3 us
    psum x1 -> x0, blocking collectives: 251 us -> none  [on_device(): sums = lax.psum(jnp.stack([kinetic, virial]), 'gx')]
    pallas_call x1, Pallas kernels: 9.92 us -> 54.9 us  [on_device(): pl.pallas_call(functools.partial(step_kernel, domains), out_shape=(rows,...]
    ppermute x5 -> x0, starting transfers between devices: 26.2 us -> none  [passed_along(): return lax.ppermute(value, axis, pairs)]
    ppermute x5 -> x0, waiting for transfers between devices: 6.61 us -> none  [passed_along(): return lax.ppermute(value, axis, pairs)]
    slice x6 -> x0, local copies, waits for them, and re-layouts: 3.87 us -> none  [the longest x1 0.76 us: on_device(): inverse_mass = atom_params[3]]
  transfers between devices with their start and end apart: 5 -> 0, of which waited for: 2 -> 0; matrix products, arithmetic and copies ran while one was open for 2% -> 0% of each run, Pallas kernels for 0% -> 0%
where the time goes in v2:
time: 59.9 us; the launch traced here: 59.5 us
  Pallas kernels  54.9 us (92%)
  local copies, waits for them, and re-layouts  3.27 us (5%)
  between operations  1.3 us (2%)
    pallas_call x1, Pallas kernels, on_device(): pl.pallas_call(functools.partial(step_kernel, domains), out_shape=(rows,...  54.9 us
    unnamed x10, local copies, waits for them, and re-layouts  3.27 us

profile of v2, /device:TPU:40, one launch (start us, length us, event | category | flops | bytes accessed | tf_op | source)
XLA Modules:
  0.0 59.5 jit_solution(788644272041447223)
XLA Ops:
  1.3 54.9 %force_step.1 = (f32[3,1536]{1,0:T(4,128)}, f32[3,1536]{1,0:T(4,128)}, f32[3,1536]{1,0:T(4,128)}, f32[4]{0:T(128)}) custom-call(s32[1]{0:T(128)S(6)} %copy.17.count_ref, f32[3]{0:T(128)} %box_ref.1, f32[4]{0:T(128)} %ext_ref.1, s32[1,96]{1,0:T(1,128)} %bitcast.1, f32[3,1536]{1,0:T(4,128)} %pos_ref.1, f32[3,1536]{1,0:T(4,128)} %vel_ref.1, f32[4,1536]{1,0:T(4,128)} %par_ref.1, ...), custom_call_target="tpu_custom_call" | custom-call | tf_op jit(solution)/shard_map/force_step/pallas_call | solution.py:362
  56.2 0.0 copy-start.1
  56.2 1.4 %copy.18 = f32[3,1536]{1,0:T(4,128)} copy(f32[3,1536]{1,0:T(4,128)} %get-tuple-element.8) | data formatting | bytes 36864
  57.6 0.0 copy-done.1
  57.6 0.0 copy-start
  57.6 0.6 %copy.19 = f32[3,1536]{1,0:T(4,128)} copy(f32[3,1536]{1,0:T(4,128)S(1)} %copy-done.1) | data formatting | bytes 36864
  58.2 0.1 copy-done
  58.3 0.0 copy-start.2
  58.3 0.6 %copy.20 = f32[3,1536]{1,0:T(4,128)} copy(f32[3,1536]{1,0:T(4,128)S(1)} %copy-done) | data formatting | bytes 36864
  58.9 0.0 copy-done.2
  59.0 0.5 copy.21
Async XLA Ops:
  56.2 1.4 %copy-start.1 = (f32[3,1536]{1,0:T(4,128)S(1)}, f32[3,1536]{1,0:T(4,128)}, u32[]{:S(2)}) copy-start(f32[3,1536]{1,0:T(4,128)} %get-tuple-element.9) | copy-start | bytes 55300
  57.6 0.7 %copy-start = (f32[3,1536]{1,0:T(4,128)S(1)}, f32[3,1536]{1,0:T(4,128)}, u32[]{:S(2)}) copy-start(f32[3,1536]{1,0:T(4,128)} %get-tuple-element.10) | copy-start | bytes 55300
  58.3 0.7 %copy-start.2 = (f32[4]{0:T(128)S(1)}, f32[4]{0:T(128)}, u32[]{:S(2)}) copy-start(f32[4]{0:T(128)} %get-tuple-element.11) | copy-start | bytes 52

commit v3 on v2

--- a/solution.py
+++ b/solution.py
@@ -50,24 +50,36 @@
 
 
 def step_kernel(
-    domains, count_ref, box_ref, ext_ref, halo_ref, pos_ref, vel_ref, par_ref, pl_ref, ex_ref,
-    force_ref, nvel_ref, npos_out, coup_ref,
-    npos_ref, npar_ref, fpos_ref, fpar_ref, fhalo_ref, near_ref, far_ref, near_in, far_in,
+    domains, count_in, box_in, ext_in, halo_in, pos_in, vel_in, par_in, pl_in, ex_in,
+    force_ref, coef_ref,
+    count_ref, box_ref, ext_ref, halo_ref, pos_ref, vel_ref, par_ref, pl_ref, ex_ref,
+    npos_ref, npar_ref, far_out, far_tab, near_force, far_force, near_in, far_in,
     part, src1, src2, sum1, sum2,
     tab_i, tab_j, jd, ri, wd, fs, acc_j, acc_i, vacc,
-    halo_send, halo_recv, force_send, force_recv, send1, recv1, send2, recv2,
+    load_sem, halo_send, halo_recv, force_send, force_recv, send1, recv1, send2, recv2, relay,
 ):
     planes = domains // PLANE
     me = lax.axis_index("gx")
     place, plane = lax.rem(me, PLANE), lax.div(me, PLANE)
     at = lambda shift: lax.rem(me + domains + shift, domains)
+    column = lambda shift: lax.rem(plane + planes + shift, planes) * PLANE + place
     mates = [plane * PLANE + lax.rem(place + k, PLANE) for k in range(1, PLANE)]
-    columns = [lax.rem(plane + k, planes) * PLANE + place for k in range(1, planes)]
+    columns = [column(k) for k in range(1, planes)]
 
     barrier = pltpu.get_barrier_semaphore()
-    greeted = [at(-1), at(-2), at(1), at(2)] + mates + columns
+    greeted = [at(-1), at(-2), at(1), at(2), column(-1), column(1)] + mates
     for other in greeted:
         pl.semaphore_signal(barrier, inc=1, device_id={"gx": other}, device_id_type=MESH)
+
+    loads = [
+        pltpu.make_async_copy(src, dst, load_sem.at[k])
+        for k, (src, dst) in enumerate((
+            (pos_in, pos_ref), (par_in, par_ref), (halo_in, halo_ref), (box_in, box_ref), (vel_in, vel_ref),
+            (count_in, count_ref), (ext_in, ext_ref), (pl_in, pl_ref), (ex_in, ex_ref),
+        ))
+    ]
+    for item in loads:
+        item.start()
 
     def copy(src, dst, send, recv, other):
         return pltpu.make_async_remote_copy(
@@ -77,12 +89,13 @@
     halo_copies = [
         copy(pos_ref, npos_ref, halo_send.at[0], halo_recv.at[0], at(-1)),
         copy(par_ref, npar_ref, halo_send.at[1], halo_recv.at[1], at(-1)),
-        copy(pos_ref, fpos_ref, halo_send.at[2], halo_recv.at[2], at(-2)),
-        copy(par_ref, fpar_ref, halo_send.at[3], halo_recv.at[3], at(-2)),
-        copy(halo_ref, fhalo_ref, halo_send.at[4], halo_recv.at[4], at(-2)),
+        copy(far_out, far_tab, halo_send.at[2], halo_recv.at[2], at(-2)),
     ]
+    for item in loads[:4]:
+        item.wait()
+
     clusters = pos_ref.shape[1] // 8
-    fars = fhalo_ref.shape[1]
+    fars = halo_ref.shape[1]
     width = fs.shape[0] * L
     box = [box_ref[c] for c in range(3)]
 
@@ -101,11 +114,35 @@
     tiles_of = clusters // 16
     half = clusters - L
     scales = (1.0, 1.0, 1.0, 1.0, 6.0, 12.0)
+    hal = jnp.concatenate(
+        [jnp.broadcast_to(halo_ref[...], (8, fars)), jnp.zeros((8, L - fars), I32)], axis=1)
     for c in range(6):
         own = to_cluster_rows(row_of(pos_ref, par_ref, c, None), clusters)
+        far_out[c] = jnp.where(hal >= L, take(own[1], hal & (L - 1)), take(own[0], hal & (L - 1)))
         for t in range(2):
             tab_i[c, :, t * L:(t + 1) * L] = own[t] * scales[c] if scales[c] != 1.0 else own[t]
             tab_j[c, :, t * L:(t + 1) * L] = own[t]
+    pl.semaphore_wait(barrier, len(greeted))
+    for item in (halo_copies[2], halo_copies[0], halo_copies[1]):
+        item.start()
+
+    def tell(round_, distance):
+        for side in (0, 1):
+            pl.semaphore_signal(
+                relay.at[2 * round_ + side], inc=1,
+                device_id={"gx": column(distance if side else -distance)}, device_id_type=MESH)
+
+    def hear(round_):
+        for side in (0, 1):
+            pl.semaphore_wait(relay.at[2 * round_ + side], 1)
+
+    distances = []
+    while 2 ** (len(distances) + 1) < planes:
+        distances.append(2 ** len(distances))
+    tell(0, distances[0])
+
+    for item in loads[4:]:
+        item.wait()
     part[...] = jnp.zeros_like(part)
     kin = None
     for t in range(tiles_of):
@@ -118,26 +155,17 @@
     vacc[...] = jnp.zeros_like(vacc)
     fs[...] = jnp.zeros_like(fs)
 
-    pl.semaphore_wait(barrier, len(greeted))
-    for item in halo_copies:
-        item.start()
     for item in halo_copies:
         item.wait()
-
     lift_near = jnp.where(me + 1 >= domains, box[0], 0.0)
     lift_far = jnp.where(me + 2 >= domains, box[0], 0.0)
-    hal = jnp.concatenate(
-        [jnp.broadcast_to(fhalo_ref[...], (8, fars)), jnp.zeros((8, L - fars), I32)], axis=1)
     for c in range(6):
         near = to_cluster_rows(row_of(npos_ref, npar_ref, c, lift_near), clusters)
-        far = to_cluster_rows(row_of(fpos_ref, fpar_ref, c, lift_far), clusters)
         rot0 = pltpu.roll(near[0], half, 1)
         rot1 = pltpu.roll(near[1], half, 1)
         tab_j[c, :, L:2 * L] = jnp.where(lane8 < half, tab_j[c, :, L:2 * L], rot0)
         tab_j[c, :, 2 * L:3 * L] = jnp.where(lane8 < half, rot0, rot1)
-        tab_j[c, :, 3 * L:4 * L] = jnp.where(
-            hal >= L, take(far[1], hal & (L - 1)), take(far[0], hal & (L - 1)))
-
+        tab_j[c, :, 3 * L:4 * L] = far_tab[c] + lift_far if c == 0 else far_tab[c]
 
     sub = iota((8, L), 0)
     count = count_ref[0]
@@ -243,33 +271,15 @@
         return carry
 
     gather(0)
-    lax.fori_loop(0, blocks, step, 0)
+    rounds = len(distances)
+    marks = [0] + [blocks - (4 + (rounds - 1 - k) * 4) for k in range(rounds)] + [blocks]
+    for k in range(rounds + 1):
+        lax.fori_loop(marks[k], marks[k + 1], step, 0)
+        if k < rounds:
+            hear(k)
+            if k + 1 < rounds:
+                tell(k + 1, distances[k + 1])
     dots(blocks - 1)
-
-    pad = jnp.zeros((24, L - half_c), F32)
-    mi = [acc_i[48 * k:48 * k + 24] + acc_i[48 * k + 24:48 * k + 48] for k in range(2)]
-    mi = [jnp.concatenate([v, pad], axis=1) for v in mi]
-    tiles = [acc_j[48 * k:48 * k + 24] + acc_j[48 * k + 24:48 * k + 48] for k in range(4)]
-    hal = jnp.concatenate([fhalo_ref[...], jnp.full((1, L - fars), 4 * L, I32)], axis=1)
-    oh_far = (jnp.broadcast_to(hal, (clusters, L)) == iota((clusters, L), 0)).astype(F32).astype(BF16)
-    ff = tiles[3]
-    f1 = ff.astype(BF16)
-    r1 = ff - f1.astype(F32)
-    f2 = r1.astype(BF16)
-    f3 = (r1 - f2.astype(F32)).astype(BF16)
-    far = sum(lax.dot_general(f, oh_far, (((1,), (1,)), ((), ())), preferred_element_type=F32) for f in (f3, f2, f1))
-    far = jnp.concatenate([far, jnp.zeros((24, 2 * L - clusters), F32)], axis=1)
-    far = [far[:, 0:L], far[:, L:]]
-    pick = sub == (lane8 & 7)
-
-    def atom_order(src, base, c, t, ref, minus=None):
-        slot = base + 16 * t
-        idx = (slot % L) + lane8 // 8
-        got = take(src[slot // L][8 * c:8 * c + 8], idx)
-        if minus is not None:
-            mine = minus[(16 * t) // half_c][8 * c:8 * c + 8]
-            got = got - take(mine, (16 * t) % half_c + lane8 // 8)
-        ref[c:c + 1, t * L:(t + 1) * L] = jnp.sum(jnp.where(pick, got, 0.0), axis=0, keepdims=True)
 
     for c in range(3):
         part[3 + c:4 + c, :] = -0.5 * jnp.sum(vacc[c], axis=0, keepdims=True)
@@ -277,23 +287,25 @@
     row = jnp.sum(jnp.where(sub == lane8, jnp.broadcast_to(sums, (8, L)), 0.0), axis=0, keepdims=True)
     src1[...] = row
     sum1[place] = src1[...]
-    for c in range(3):
-        for t in range(tiles_of):
-            atom_order(tiles, clusters, c, t, near_ref)
     plane_copies = [
         copy(src1, sum1.at[place], send1.at[k], recv1.at[place], mate) for k, mate in enumerate(mates)]
     for item in plane_copies:
         item.start()
-    for c in range(3):
-        for t in range(tiles_of):
-            atom_order(far, 0, c, t, far_ref)
-    near_copy = copy(near_ref, near_in, force_send.at[0], force_recv.at[0], at(1))
+    tile_at = lambda k: acc_j[48 * k:48 * k + 24] + acc_j[48 * k + 24:48 * k + 48]
+    near_force[0] = tile_at(1)
+    near_force[1] = tile_at(2)
+    far_force[...] = tile_at(3)
+    tiles = [tile_at(0), near_force[0]]
+    pad = jnp.zeros((24, L - half_c), F32)
+    mi = [acc_i[48 * k:48 * k + 24] + acc_i[48 * k + 24:48 * k + 48] for k in range(2)]
+    mi = [jnp.concatenate([v, pad], axis=1) for v in mi]
+    hal1 = jnp.concatenate([halo_ref[...], jnp.full((1, L - fars), 4 * L, I32)], axis=1)
+    oh_far = (jnp.broadcast_to(hal1, (clusters, L)) == iota((clusters, L), 0)).astype(F32).astype(BF16)
+    near_copy = copy(near_force, near_in, force_send.at[0], force_recv.at[0], at(1))
+    far_copy = copy(far_force, far_in, force_send.at[1], force_recv.at[1], at(2))
     near_copy.start()
-    for c in range(3):
-        for t in range(tiles_of):
-            atom_order(tiles, 0, c, t, force_ref, mi)
-    far_copy = copy(far_ref, far_in, force_send.at[1], force_recv.at[1], at(2))
     far_copy.start()
+
     for k in range(1, PLANE):
         other = lax.rem(place + k, PLANE)
         copy(src1, sum1.at[other], send1.at[k - 1], recv1.at[other], mates[k - 1]).wait_recv()
@@ -306,9 +318,26 @@
         copy(src2, sum2.at[plane], send2.at[k], recv2.at[plane], other) for k, other in enumerate(columns)]
     for item in column_copies:
         item.start()
+
     near_copy.wait()
     far_copy.wait()
-    force_ref[...] = force_ref[...] + near_in[...] + far_in[...]
+    ff = far_in[...]
+    f1 = ff.astype(BF16)
+    r1 = ff - f1.astype(F32)
+    f2 = r1.astype(BF16)
+    f3 = (r1 - f2.astype(F32)).astype(BF16)
+    far = sum(lax.dot_general(f, oh_far, (((1,), (1,)), ((), ())), preferred_element_type=F32) for f in (f3, f2, f1))
+    tiles[0] = tiles[0] + far[:, 0:L]
+    tiles[1] = tiles[1] + jnp.concatenate([far[:, L:], jnp.zeros((24, 2 * L - clusters), F32)], axis=1)
+    back = [near_in[0], near_in[1]]
+    pick = sub == (lane8 & 7)
+    for c in range(3):
+        for t in range(tiles_of):
+            def window(tabs, slot, size):
+                return take(tabs[slot // size][8 * c:8 * c + 8], slot % size + lane8 // 8)
+            got = window(tiles, 16 * t, L) - window(mi, 16 * t, half_c) + window(back, half + 16 * t, L)
+            force_ref[c:c + 1, t * L:(t + 1) * L] = jnp.sum(jnp.where(pick, got, 0.0), axis=0, keepdims=True)
+
     for item in plane_copies:
         item.wait_send()
     for k in range(1, planes):
@@ -322,22 +351,29 @@
     total = one_of[0] + one_of[1] + one_of[2]
     volume = box[0] * box[1] * box[2]
     ratio = 2.0 * total / (3.0 * (8 * clusters * domains) * thermal_scale_unit)
-    damping = ext_ref[0] + reservoir_inertia_mass * (ratio - 1.0)
-    coup_ref[0] = damping[0, 0]
+    coef = ext_ref[0] + reservoir_inertia_mass * (ratio - 1.0)
     for c in range(3):
         rate = ext_ref[1 + c] + barostat_gain * (
             one_of[c] - one_of[3 + c] - pressure_target * volume / 2.0
         ) / (total / 3.0)
-        coup_ref[1 + c] = rate[0, 0]
-        drag, grow = (damping + rate)[0:1], (1.0 + time_step * rate)[0:1]
-        for t in range(tiles_of):
-            cols = slice(t * L, (t + 1) * L)
-            v = vel_ref[c:c + 1, cols]
-            v = v + time_step * (force_ref[c:c + 1, cols] * par_ref[3:4, cols] - drag * v)
-            nvel_ref[c:c + 1, cols] = v
-            npos_out[c:c + 1, cols] = pos_ref[c:c + 1, cols] * grow + time_step * v
+        coef = jnp.where(sub == 1 + c, rate, coef)
+    coef_ref[...] = coef
     for item in column_copies:
         item.wait_send()
+
+
+def update_kernel(force_in, coef_ref, pos_ref, vel_ref, par_ref, force_ref, nvel_ref, npos_ref, coup_ref):
+    coef = coef_ref[...]
+    for k in range(4):
+        coup_ref[k] = coef[k, 0]
+    drag, grow = coef[0:1] + coef[1:4], 1.0 + time_step * coef[1:4]
+    for t in range(pos_ref.shape[1] // L):
+        cols = slice(t * L, (t + 1) * L)
+        f, v = force_in[:, cols], vel_ref[:, cols]
+        v = v + time_step * (f * par_ref[3:4, cols] - drag * v)
+        force_ref[:, cols] = f
+        nvel_ref[:, cols] = v
+        npos_ref[:, cols] = pos_ref[:, cols] * grow + time_step * v
 
 
 def on_device(
@@ -355,25 +391,32 @@
     planes = domains // PLANE
     atoms, fars = positions.shape[1], halo_far.shape[0]
     clusters, groups = atoms // 8, WIDTH // L
-    smem = pl.BlockSpec(memory_space=pltpu.SMEM)
     vmem = pl.BlockSpec(memory_space=pltpu.VMEM)
     rows = jax.ShapeDtypeStruct((3, atoms), F32)
     dma = pltpu.SemaphoreType.DMA
-    return pl.pallas_call(
+    forces, coef = pl.pallas_call(
         functools.partial(step_kernel, domains),
-        out_shape=(rows, rows, rows, jax.ShapeDtypeStruct((4,), F32)),
-        in_specs=[smem] * 3 + [vmem] * 6,
-        out_specs=(vmem, vmem, vmem, smem),
+        out_shape=(rows, jax.ShapeDtypeStruct((8, L), F32)),
+        in_specs=[pl.BlockSpec(memory_space=pltpu.HBM)] * 9,
+        out_specs=(vmem, vmem),
         scratch_shapes=[
-            pltpu.VMEM((3, atoms), F32),
-            pltpu.VMEM((4, atoms), F32),
-            pltpu.VMEM((3, atoms), F32),
-            pltpu.VMEM((4, atoms), F32),
+            pltpu.SMEM((1,), I32),
+            pltpu.SMEM((3,), F32),
+            pltpu.SMEM((4,), F32),
             pltpu.VMEM((1, fars), I32),
             pltpu.VMEM((3, atoms), F32),
             pltpu.VMEM((3, atoms), F32),
+            pltpu.VMEM((4, atoms), F32),
+            pltpu.VMEM(pair_list.shape, I32),
+            pltpu.VMEM(exclusion.shape, I32),
             pltpu.VMEM((3, atoms), F32),
-            pltpu.VMEM((3, atoms), F32),
+            pltpu.VMEM((4, atoms), F32),
+            pltpu.VMEM((6, 8, L), F32),
+            pltpu.VMEM((6, 8, L), F32),
+            pltpu.VMEM((2, 24, L), F32),
+            pltpu.VMEM((24, L), F32),
+            pltpu.VMEM((2, 24, L), F32),
+            pltpu.VMEM((24, L), F32),
             pltpu.VMEM((8, L), F32),
             pltpu.VMEM((1, L), F32),
             pltpu.VMEM((1, L), F32),
@@ -388,19 +431,28 @@
             pltpu.VMEM((192, L), F32),
             pltpu.VMEM((96, clusters // 2), F32),
             pltpu.VMEM((3, 8, L), F32),
-            dma((5,)),
-            dma((5,)),
+            dma((9,)),
+            dma((3,)),
+            dma((3,)),
             dma((2,)),
             dma((2,)),
             dma((PLANE - 1,)),
             dma((PLANE,)),
             dma((planes - 1,)),
             dma((planes,)),
+            pltpu.SemaphoreType.REGULAR((2 * planes.bit_length(),)),
         ],
         compiler_params=pltpu.CompilerParams(collective_id=0, has_side_effects=True),
         name="force_step",
     )(pair_count, box_lengths, extended_variables, halo_far[None], positions, velocities, atom_params,
       pair_list, exclusion)
+    return pl.pallas_call(
+        update_kernel,
+        out_shape=(rows, rows, rows, jax.ShapeDtypeStruct((4,), F32)),
+        in_specs=[vmem] * 5,
+        out_specs=(vmem, vmem, vmem, pl.BlockSpec(memory_space=pltpu.SMEM)),
+        name="update",
+    )(forces, coef, positions, velocities, atom_params)
 
 
 def solution(mesh):

time: 59.9 us -> 56.2 us (0.938)
  local copies, waits for them, and re-layouts: 3.27 us -> 0 us
    unnamed x10 -> x0, local copies, waits for them, and re-layouts: 3.27 us -> none
    pallas_call x1, Pallas kernels: 54.9 us -> 53.2 us  [on_device(): pl.pallas_call(functools.partial(step_kernel, domains), out_shape=(rows,...]
    pallas_call x0 -> x1, Pallas kernels: none -> 1.45 us  [on_device(): pl.pallas_call(update_kernel, out_shape=(rows, rows, rows, jax.ShapeDtype...]
where the time goes in v3:
time: 56.2 us; the launch traced here: 56 us
  Pallas kernels  54.7 us (97%)
  between operations  1.29 us (2%)
    pallas_call x1, Pallas kernels, on_device(): pl.pallas_call(functools.partial(step_kernel, domains), out_shape=(rows,...  53.2 us
    pallas_call x1, Pallas kernels, on_device(): pl.pallas_call(update_kernel, out_shape=(rows, rows, rows, jax.ShapeDtype...  1.45 us

profile of v3, /device:TPU:40, one launch (start us, length us, event | category | flops | bytes accessed | tf_op | source)
XLA Modules:
  0.0 56.0 jit_solution(7826937982423000744)
XLA Ops:
  1.3 53.2 %force_step.1 = (f32[3,1536]{1,0:T(4,128)}, f32[8,128]{1,0:T(8,128)}) custom-call(s32[1]{0:T(128)S(6)} %copy.13.count_in, f32[3]{0:T(128)} %box_in.1, f32[4]{0:T(128)} %ext_in.1, s32[1,96]{1,0:T(1,128)} %bitcast.1, f32[3,1536]{1,0:T(4,128)} %pos_ref.1, f32[3,1536]{1,0:T(4,128)} %vel_ref.1, f32[4,1536]{1,0:T(4,128)} %par_ref.1, s32[3,16896]{1,0:T(4,128)} %pl_in.1, ...), custom_call_target="tpu_custom_call" | custom-call | tf_op jit(solution)/shard_map/force_step/pallas_call | solution.py:397
  54.5 1.4 %update.1 = (f32[3,1536]{1,0:T(4,128)}, f32[3,1536]{1,0:T(4,128)}, f32[3,1536]{1,0:T(4,128)}, f32[4]{0:T(128)}) custom-call(f32[3,1536]{1,0:T(4,128)} %get-tuple-element.6.force_in, f32[8,128]{1,0:T(8,128)} %get-tuple-element.7.coef_ref, f32[3,1536]{1,0:T(4,128)} %pos_ref.1, f32[3,1536]{1,0:T(4,128)} %vel_ref.1, f32[4,1536]{1,0:T(4,128)} %par_ref.1), custom_call_target="tpu_custom_call" | custom-call | tf_op jit(solution)/shard_map/update/pallas_call | solution.py:449

commit v4 on v3

--- a/solution.py
+++ b/solution.py
@@ -64,10 +64,11 @@
     at = lambda shift: lax.rem(me + domains + shift, domains)
     column = lambda shift: lax.rem(plane + planes + shift, planes) * PLANE + place
     mates = [plane * PLANE + lax.rem(place + k, PLANE) for k in range(1, PLANE)]
-    columns = [column(k) for k in range(1, planes)]
+    steps = sorted(range(1, planes), key=lambda k: min(k, planes - k))
+    columns = [column(k) for k in steps]
 
     barrier = pltpu.get_barrier_semaphore()
-    greeted = [at(-1), at(-2), at(1), at(2), column(-1), column(1)] + mates
+    greeted = [at(2), at(1), at(-1), at(-2), column(1), column(-1)] + mates
     for other in greeted:
         pl.semaphore_signal(barrier, inc=1, device_id={"gx": other}, device_id_type=MESH)
 
@@ -272,13 +273,12 @@
 
     gather(0)
     rounds = len(distances)
-    marks = [0] + [blocks - (4 + (rounds - 1 - k) * 4) for k in range(rounds)] + [blocks]
-    for k in range(rounds + 1):
+    marks = [0] + [5 + 7 * k for k in range(rounds - 1)] + [blocks]
+    for k in range(rounds):
         lax.fori_loop(marks[k], marks[k + 1], step, 0)
-        if k < rounds:
+        if k + 1 < rounds:
             hear(k)
-            if k + 1 < rounds:
-                tell(k + 1, distances[k + 1])
+            tell(k + 1, distances[k + 1])
     dots(blocks - 1)
 
     for c in range(3):
@@ -306,6 +306,7 @@
     near_copy.start()
     far_copy.start()
 
+    hear(rounds - 1)
     for k in range(1, PLANE):
         other = lax.rem(place + k, PLANE)
         copy(src1, sum1.at[other], send1.at[k - 1], recv1.at[other], mates[k - 1]).wait_recv()
@@ -340,9 +341,9 @@
 
     for item in plane_copies:
         item.wait_send()
-    for k in range(1, planes):
-        other = lax.rem(plane + k, planes)
-        copy(src2, sum2.at[other], send2.at[k - 1], recv2.at[other], columns[k - 1]).wait_recv()
+    for k, step_ in enumerate(steps):
+        other = lax.rem(plane + step_, planes)
+        copy(src2, sum2.at[other], send2.at[k], recv2.at[other], columns[k]).wait_recv()
     row = sum2[0]
     for k in range(1, planes):
         row = row + sum2[k]

time: 56.2 us -> 50.9 us (0.906)
  Pallas kernels: 54.7 us -> 49.4 us
    pallas_call x1, Pallas kernels: 53.2 us -> 48 us  [on_device(): pl.pallas_call(functools.partial(step_kernel, domains), out_shape=(rows,...]
where the time goes in v4:
time: 50.9 us; the launch traced here: 50.7 us
  Pallas kernels  49.4 us (97%)
  between operations  1.29 us (3%)
    pallas_call x1, Pallas kernels, on_device(): pl.pallas_call(functools.partial(step_kernel, domains), out_shape=(rows,...  48 us
    pallas_call x1, Pallas kernels, on_device(): pl.pallas_call(update_kernel, out_shape=(rows, rows, rows, jax.ShapeDtype...  1.45 us

profile of v4, /device:TPU:40, one launch (start us, length us, event | category | flops | bytes accessed | tf_op | source)
XLA Modules:
  0.0 50.7 jit_solution(3130010595829776843)
XLA Ops:
  1.3 48.0 %force_step.1 = (f32[3,1536]{1,0:T(4,128)}, f32[8,128]{1,0:T(8,128)}) custom-call(s32[1]{0:T(128)S(6)} %copy.13.count_in, f32[3]{0:T(128)} %box_in.1, f32[4]{0:T(128)} %ext_in.1, s32[1,96]{1,0:T(1,128)} %bitcast.1, f32[3,1536]{1,0:T(4,128)} %pos_ref.1, f32[3,1536]{1,0:T(4,128)} %vel_ref.1, f32[4,1536]{1,0:T(4,128)} %par_ref.1, s32[3,16896]{1,0:T(4,128)} %pl_in.1, ...), custom_call_target="tpu_custom_call" | custom-call | tf_op jit(solution)/shard_map/force_step/pallas_call | solution.py:398
  49.3 1.4 %update.1 = (f32[3,1536]{1,0:T(4,128)}, f32[3,1536]{1,0:T(4,128)}, f32[3,1536]{1,0:T(4,128)}, f32[4]{0:T(128)}) custom-call(f32[3,1536]{1,0:T(4,128)} %get-tuple-element.6.force_in, f32[8,128]{1,0:T(8,128)} %get-tuple-element.7.coef_ref, f32[3,1536]{1,0:T(4,128)} %pos_ref.1, f32[3,1536]{1,0:T(4,128)} %vel_ref.1, f32[4,1536]{1,0:T(4,128)} %par_ref.1), custom_call_target="tpu_custom_call" | custom-call | tf_op jit(solution)/shard_map/update/pallas_call | solution.py:450

commit v5 on v4

--- a/solution.py
+++ b/solution.py
@@ -53,7 +53,7 @@
     domains, count_in, box_in, ext_in, halo_in, pos_in, vel_in, par_in, pl_in, ex_in,
     force_ref, coef_ref,
     count_ref, box_ref, ext_ref, halo_ref, pos_ref, vel_ref, par_ref, pl_ref, ex_ref,
-    npos_ref, npar_ref, far_out, far_tab, near_force, far_force, near_in, far_in,
+    near_out, mix_out, far_out, mix_in, near_force, far_force, near_in, far_in,
     part, src1, src2, sum1, sum2,
     tab_i, tab_j, jd, ri, wd, fs, acc_j, acc_i, vacc,
     load_sem, halo_send, halo_recv, force_send, force_recv, send1, recv1, send2, recv2, relay,
@@ -88,9 +88,9 @@
         )
 
     halo_copies = [
-        copy(pos_ref, npos_ref, halo_send.at[0], halo_recv.at[0], at(-1)),
-        copy(par_ref, npar_ref, halo_send.at[1], halo_recv.at[1], at(-1)),
-        copy(far_out, far_tab, halo_send.at[2], halo_recv.at[2], at(-2)),
+        copy(near_out, tab_j.at[2], halo_send.at[0], halo_recv.at[0], at(-1)),
+        copy(mix_out, mix_in, halo_send.at[1], halo_recv.at[1], at(-1)),
+        copy(far_out, tab_j.at[3], halo_send.at[2], halo_recv.at[2], at(-2)),
     ]
     for item in loads[:4]:
         item.wait()
@@ -100,15 +100,10 @@
     width = fs.shape[0] * L
     box = [box_ref[c] for c in range(3)]
 
-    def row_of(pref, qref, c, lift):
+    def row_of(c):
         def row(start):
-            if c < 3:
-                r = pref[pl.ds(c, 1), pl.ds(start, L)]
-                if c == 0 and lift is not None:
-                    r = r + lift
-            else:
-                r = qref[pl.ds(c - 3, 1), pl.ds(start, L)]
-            return jnp.broadcast_to(r, (8, L))
+            ref, r = (pos_ref, c) if c < 3 else (par_ref, c - 3)
+            return jnp.broadcast_to(ref[pl.ds(r, 1), pl.ds(start, L)], (8, L))
         return row
 
     lane8 = iota((8, L), 1)
@@ -117,14 +112,25 @@
     scales = (1.0, 1.0, 1.0, 1.0, 6.0, 12.0)
     hal = jnp.concatenate(
         [jnp.broadcast_to(halo_ref[...], (8, fars)), jnp.zeros((8, L - fars), I32)], axis=1)
+    lifts = [jnp.where(me < k, box[0], 0.0) for k in (1, 2)]
+    heads = []
     for c in range(6):
-        own = to_cluster_rows(row_of(pos_ref, par_ref, c, None), clusters)
-        far_out[c] = jnp.where(hal >= L, take(own[1], hal & (L - 1)), take(own[0], hal & (L - 1)))
+        own = to_cluster_rows(row_of(c), clusters)
         for t in range(2):
             tab_i[c, :, t * L:(t + 1) * L] = own[t] * scales[c] if scales[c] != 1.0 else own[t]
-            tab_j[c, :, t * L:(t + 1) * L] = own[t]
+            tab_j[t, c] = own[t]
+        far = jnp.where(hal >= L, take(own[1], hal & (L - 1)), take(own[0], hal & (L - 1)))
+        far_out[c] = far + lifts[1] if c == 0 else far
+        if c == 0:
+            own = [v + lifts[0] for v in own]
+        rot0, rot1 = pltpu.roll(own[0], half, 1), pltpu.roll(own[1], half, 1)
+        near_out[c] = jnp.where(lane8 < half, rot0, rot1)
+        if c < 3:
+            heads.append(rot0)
+        else:
+            mix_out[c - 3] = jnp.where(lane8 < half, own[0], heads[c - 3])
     pl.semaphore_wait(barrier, len(greeted))
-    for item in (halo_copies[2], halo_copies[0], halo_copies[1]):
+    for item in halo_copies:
         item.start()
 
     def tell(round_, distance):
@@ -158,15 +164,10 @@
 
     for item in halo_copies:
         item.wait()
-    lift_near = jnp.where(me + 1 >= domains, box[0], 0.0)
-    lift_far = jnp.where(me + 2 >= domains, box[0], 0.0)
-    for c in range(6):
-        near = to_cluster_rows(row_of(npos_ref, npar_ref, c, lift_near), clusters)
-        rot0 = pltpu.roll(near[0], half, 1)
-        rot1 = pltpu.roll(near[1], half, 1)
-        tab_j[c, :, L:2 * L] = jnp.where(lane8 < half, tab_j[c, :, L:2 * L], rot0)
-        tab_j[c, :, 2 * L:3 * L] = jnp.where(lane8 < half, rot0, rot1)
-        tab_j[c, :, 3 * L:4 * L] = far_tab[c] + lift_far if c == 0 else far_tab[c]
+    for c in range(3):
+        mixed = mix_in[c]
+        tab_j[1, c] = jnp.where(lane8 < half, tab_j[1, c], mixed)
+        tab_j[1, c + 3] = jnp.where(lane8 < half, tab_j[1, c + 3], pltpu.roll(mixed, half, 1))
 
     sub = iota((8, L), 0)
     count = count_ref[0]
@@ -176,7 +177,7 @@
     zero16 = jnp.zeros((16, L), BF16)
 
     groups = width // L
-    base16 = iota((16, L), 0).astype(I16)
+    bases = [(iota((16, L), 0) + 16 * r).astype(I16) for r in range(L // 16)]
 
     def gather(block):
         for g in range(groups):
@@ -199,7 +200,7 @@
                     v = v - jnp.where(above_y if c == 1 else s3 == 2, box[c], 0.0)
                 ri[g, c] = v
             for c in range(6):
-                q = [take(tab_j[c, :, t * L:(t + 1) * L], jl) for t in range(4)]
+                q = [take(tab_j[t, c], jl) for t in range(4)]
                 v = jnp.where(jh, jnp.where(jm, q[3], q[2]), jnp.where(jm, q[1], q[0]))
                 if c in (1, 2):
                     v = v - jnp.where(below_y if c == 1 else s3 == 0, box[c], 0.0)
@@ -256,8 +257,8 @@
                 [jnp.where(later, zero16, p) for p in parts(ti)] + [jnp.where(later, p, zero16) for p in parts(ti)], axis=0))
             j16 = j16 & (L - 1)
             i16 = jnp.where(later, i16 - half_c, i16)
-            ojs.append(jnp.concatenate([jnp.where(base16 == j16 - 16 * r, one16, zero16) for r in range(L // 16)], axis=0))
-            ois.append(jnp.concatenate([jnp.where(base16 == i16 - 16 * r, one16, zero16) for r in range(half_c // 16)], axis=0))
+            ojs.append(jnp.concatenate([jnp.where(bases[r] == j16, one16, zero16) for r in range(L // 16)], axis=0))
+            ois.append(jnp.concatenate([jnp.where(bases[r] == i16, one16, zero16) for r in range(half_c // 16)], axis=0))
         contract = (((1,), (1,)), ((), ()))
         wide = lambda xs: jnp.concatenate(xs, axis=1)
         acc_j[...] += lax.dot_general(wide(tjs), wide(ojs), contract, preferred_element_type=F32)
@@ -279,8 +280,6 @@
         if k + 1 < rounds:
             hear(k)
             tell(k + 1, distances[k + 1])
-    dots(blocks - 1)
-
     for c in range(3):
         part[3 + c:4 + c, :] = -0.5 * jnp.sum(vacc[c], axis=0, keepdims=True)
     sums = jnp.sum(part[...], axis=1, keepdims=True)
@@ -291,20 +290,21 @@
         copy(src1, sum1.at[place], send1.at[k], recv1.at[place], mate) for k, mate in enumerate(mates)]
     for item in plane_copies:
         item.start()
+    dots(blocks - 1)
     tile_at = lambda k: acc_j[48 * k:48 * k + 24] + acc_j[48 * k + 24:48 * k + 48]
     near_force[0] = tile_at(1)
     near_force[1] = tile_at(2)
     far_force[...] = tile_at(3)
+    near_copy = copy(near_force, near_in, force_send.at[0], force_recv.at[0], at(1))
+    far_copy = copy(far_force, far_in, force_send.at[1], force_recv.at[1], at(2))
+    far_copy.start()
+    near_copy.start()
     tiles = [tile_at(0), near_force[0]]
     pad = jnp.zeros((24, L - half_c), F32)
     mi = [acc_i[48 * k:48 * k + 24] + acc_i[48 * k + 24:48 * k + 48] for k in range(2)]
     mi = [jnp.concatenate([v, pad], axis=1) for v in mi]
     hal1 = jnp.concatenate([halo_ref[...], jnp.full((1, L - fars), 4 * L, I32)], axis=1)
     oh_far = (jnp.broadcast_to(hal1, (clusters, L)) == iota((clusters, L), 0)).astype(F32).astype(BF16)
-    near_copy = copy(near_force, near_in, force_send.at[0], force_recv.at[0], at(1))
-    far_copy = copy(far_force, far_in, force_send.at[1], force_recv.at[1], at(2))
-    near_copy.start()
-    far_copy.start()
 
     hear(rounds - 1)
     for k in range(1, PLANE):
@@ -410,10 +410,10 @@
             pltpu.VMEM((4, atoms), F32),
             pltpu.VMEM(pair_list.shape, I32),
             pltpu.VMEM(exclusion.shape, I32),
-            pltpu.VMEM((3, atoms), F32),
-            pltpu.VMEM((4, atoms), F32),
             pltpu.VMEM((6, 8, L), F32),
+            pltpu.VMEM((3, 8, L), F32),
             pltpu.VMEM((6, 8, L), F32),
+            pltpu.VMEM((3, 8, L), F32),
             pltpu.VMEM((2, 24, L), F32),
             pltpu.VMEM((24, L), F32),
             pltpu.VMEM((2, 24, L), F32),
@@ -424,7 +424,7 @@
             pltpu.VMEM((PLANE, 1, L), F32),
             pltpu.VMEM((planes, 1, L), F32),
             pltpu.VMEM((6, 8, 2 * L), F32),
-            pltpu.VMEM((6, 8, 4 * L), F32),
+            pltpu.VMEM((4, 6, 8, L), F32),
             pltpu.VMEM((groups, 6, 16, L), F32),
             pltpu.VMEM((groups, 6, 8, L), F32),
             pltpu.VMEM((groups, 8, L), I32),
@@ -443,15 +443,17 @@
             dma((planes,)),
             pltpu.SemaphoreType.REGULAR((2 * planes.bit_length(),)),
         ],
-        compiler_params=pltpu.CompilerParams(collective_id=0, has_side_effects=True),
+        compiler_params=pltpu.CompilerParams(
+            collective_id=0, has_side_effects=True, vmem_limit_bytes=50000 * 1024),
         name="force_step",
-    )(pair_count, box_lengths, extended_variables, halo_far[None], positions, velocities, atom_params,
-      pair_list, exclusion)
+    )(pair_count, *[pltpu.with_memory_space_constraint(x, pltpu.HBM) for x in (box_lengths, extended_variables, halo_far[None], positions, velocities, atom_params,
+      pair_list, exclusion)])
     return pl.pallas_call(
         update_kernel,
         out_shape=(rows, rows, rows, jax.ShapeDtypeStruct((4,), F32)),
         in_specs=[vmem] * 5,
         out_specs=(vmem, vmem, vmem, pl.BlockSpec(memory_space=pltpu.SMEM)),
+        compiler_params=pltpu.CompilerParams(vmem_limit_bytes=8000 * 1024),
         name="update",
     )(forces, coef, positions, velocities, atom_params)
 

time: 50.9 us -> 49.7 us (0.976)
  Pallas kernels: 49.4 us -> 48.1 us
    pallas_call x1, Pallas kernels: 1.45 us -> 0.65 us  [on_device(): pl.pallas_call(update_kernel, out_shape=(rows, rows, rows, jax.ShapeDtype...]
    pallas_call x1, Pallas kernels: 48 us -> 47.4 us  [on_device(): pl.pallas_call(functools.partial(step_kernel, domains), out_shape=(rows,...]
where the time goes in v5:
time: 49.7 us; the launch traced here: 49.4 us
  Pallas kernels  48.1 us (97%)
  between operations  1.33 us (3%)
    pallas_call x1, Pallas kernels, on_device(): pl.pallas_call(functools.partial(step_kernel, domains), out_shape=(rows,...  47.4 us

profile of v5, /device:TPU:40, one launch (start us, length us, event | category | flops | bytes accessed | tf_op | source)
XLA Modules:
  0.0 49.4 jit_solution(1209978051094367842)
XLA Ops:
  1.3 0.0 copy-start
  1.3 0.0 copy-start.1
  1.3 0.0 copy-start.2
  1.3 47.4 %force_step.1 = (f32[3,1536]{1,0:T(4,128)S(1)}, f32[8,128]{1,0:T(8,128)S(1)}) custom-call(s32[1]{0:T(128)S(6)} %copy.13.count_in, f32[3]{0:T(128)} %box_in.1, f32[4]{0:T(128)} %ext_in.1, s32[1,96]{1,0:T(1,128)} %bitcast.1, f32[3,1536]{1,0:T(4,128)} %pos_ref.1, f32[3,1536]{1,0:T(4,128)} %vel_ref.1, f32[4,1536]{1,0:T(4,128)} %par_ref.1, s32[3,16896]{1,0:T(4,128)} %pl_in.1, ...), custom_call_target="tpu_custom_call" | custom-call | tf_op jit(solution)/shard_map/force_step/pallas_call | solution.py:398
  48.7 0.0 copy-done
  48.8 0.0 copy-done.1
  48.8 0.0 copy-done.2
  48.8 0.7 %update.1 = (f32[3,1536]{1,0:T(4,128)}, f32[3,1536]{1,0:T(4,128)}, f32[3,1536]{1,0:T(4,128)}, f32[4]{0:T(128)}) custom-call(f32[3,1536]{1,0:T(4,128)S(1)} %get-tuple-element.6.force_in, f32[8,128]{1,0:T(8,128)S(1)} %get-tuple-element.7.coef_ref, f32[3,1536]{1,0:T(4,128)S(1)} %copy-done, f32[3,1536]{1,0:T(4,128)S(1)} %copy-done.1, f32[4,1536]{1,0:T(4,128)S(1)} %copy-done.2), custom_call_target="tpu_custom_call" | custom-call | tf_op jit(solution)/shard_map/update/pallas_call | solution.py:451
Async XLA Ops:
  1.3 47.5 %copy-start = (f32[3,1536]{1,0:T(4,128)S(1)}, f32[3,1536]{1,0:T(4,128)}, u32[]{:S(2)}) copy-start(f32[3,1536]{1,0:T(4,128)} %pos_ref.1) | copy-start | bytes 55300
  1.3 47.5 %copy-start.1 = (f32[3,1536]{1,0:T(4,128)S(1)}, f32[3,1536]{1,0:T(4,128)}, u32[]{:S(2)}) copy-start(f32[3,1536]{1,0:T(4,128)} %vel_ref.1) | copy-start | bytes 55300
  1.3 47.5 %copy-start.2 = (f32[4,1536]{1,0:T(4,128)S(1)}, f32[4,1536]{1,0:T(4,128)}, u32[]{:S(2)}) copy-start(f32[4,1536]{1,0:T(4,128)} %par_ref.1) | copy-start | bytes 73732

commit v6 on v5

--- a/solution.py
+++ b/solution.py
@@ -54,9 +54,9 @@
     force_ref, coef_ref,
     count_ref, box_ref, ext_ref, halo_ref, pos_ref, vel_ref, par_ref, pl_ref, ex_ref,
     near_out, mix_out, far_out, mix_in, near_force, far_force, near_in, far_in,
-    part, src1, src2, sum1, sum2,
+    part, src1, src2, sum1, prev1, sum2,
     tab_i, tab_j, jd, ri, wd, fs, acc_j, acc_i, vacc,
-    load_sem, halo_send, halo_recv, force_send, force_recv, send1, recv1, send2, recv2, relay,
+    load_sem, halo_send, halo_recv, force_send, force_recv, send1, recv1, send3, recv3, send2, recv2, relay,
 ):
     planes = domains // PLANE
     me = lax.axis_index("gx")
@@ -64,7 +64,7 @@
     at = lambda shift: lax.rem(me + domains + shift, domains)
     column = lambda shift: lax.rem(plane + planes + shift, planes) * PLANE + place
     mates = [plane * PLANE + lax.rem(place + k, PLANE) for k in range(1, PLANE)]
-    steps = sorted(range(1, planes), key=lambda k: min(k, planes - k))
+    steps = sorted(range(2, planes), key=lambda k: min(k, planes - k))
     columns = [column(k) for k in steps]
 
     barrier = pltpu.get_barrier_semaphore()
@@ -274,7 +274,7 @@
 
     gather(0)
     rounds = len(distances)
-    marks = [0] + [5 + 7 * k for k in range(rounds - 1)] + [blocks]
+    marks = [0] + [3 + 15 * k for k in range(rounds - 1)] + [blocks]
     for k in range(rounds):
         lax.fori_loop(marks[k], marks[k + 1], step, 0)
         if k + 1 < rounds:
@@ -288,6 +288,10 @@
     sum1[place] = src1[...]
     plane_copies = [
         copy(src1, sum1.at[place], send1.at[k], recv1.at[place], mate) for k, mate in enumerate(mates)]
+    above = lax.rem(plane + 1, planes) * PLANE
+    plane_copies += [
+        copy(src1, prev1.at[place], send3.at[k], recv3.at[place], above + lax.rem(place + k, PLANE))
+        for k in range(PLANE)]
     for item in plane_copies:
         item.start()
     dots(blocks - 1)
@@ -320,6 +324,7 @@
     for item in column_copies:
         item.start()
 
+    below = lax.rem(plane + planes - 1, planes)
     near_copy.wait()
     far_copy.wait()
     ff = far_in[...]
@@ -341,8 +346,15 @@
 
     for item in plane_copies:
         item.wait_send()
+    for k in range(PLANE):
+        other = lax.rem(place + k, PLANE)
+        copy(src1, prev1.at[other], send3.at[k], recv3.at[other], below * PLANE + other).wait_recv()
+    row = prev1[0]
+    for k in range(1, PLANE):
+        row = row + prev1[k]
+    sum2[below] = row
     for k, step_ in enumerate(steps):
-        other = lax.rem(plane + step_, planes)
+        other = lax.rem(plane + planes - step_, planes)
         copy(src2, sum2.at[other], send2.at[k], recv2.at[other], columns[k]).wait_recv()
     row = sum2[0]
     for k in range(1, planes):
@@ -422,6 +434,7 @@
             pltpu.VMEM((1, L), F32),
             pltpu.VMEM((1, L), F32),
             pltpu.VMEM((PLANE, 1, L), F32),
+            pltpu.VMEM((PLANE, 1, L), F32),
             pltpu.VMEM((planes, 1, L), F32),
             pltpu.VMEM((6, 8, 2 * L), F32),
             pltpu.VMEM((4, 6, 8, L), F32),
@@ -439,7 +452,9 @@
             dma((2,)),
             dma((PLANE - 1,)),
             dma((PLANE,)),
-            dma((planes - 1,)),
+            dma((PLANE,)),
+            dma((PLANE,)),
+            dma((planes - 2,)),
             dma((planes,)),
             pltpu.SemaphoreType.REGULAR((2 * planes.bit_length(),)),
         ],

time: 49.7 us -> 49 us (0.986)
  Pallas kernels: 48.1 us -> 47.5 us
    pallas_call x1, Pallas kernels: 47.4 us -> 46.8 us  [on_device(): pl.pallas_call(functools.partial(step_kernel, domains), out_shape=(rows,...]
where the time goes in v6:
time: 49 us; the launch traced here: 48.8 us
  Pallas kernels  47.5 us (97%)
  between operations  1.33 us (3%)
    pallas_call x1, Pallas kernels, on_device(): pl.pallas_call(functools.partial(step_kernel, domains), out_shape=(rows,...  46.8 us

profile of v6, /device:TPU:40, one launch (start us, length us, event | category | flops | bytes accessed | tf_op | source)
XLA Modules:
  0.0 48.8 jit_solution(13628292901182540800)
XLA Ops:
  1.3 0.0 copy-start
  1.3 0.0 copy-start.1
  1.3 0.0 copy-start.2
  1.3 46.8 %force_step.1 = (f32[3,1536]{1,0:T(4,128)S(1)}, f32[8,128]{1,0:T(8,128)S(1)}) custom-call(s32[1]{0:T(128)S(6)} %copy.13.count_in, f32[3]{0:T(128)} %box_in.1, f32[4]{0:T(128)} %ext_in.1, s32[1,96]{1,0:T(1,128)} %bitcast.1, f32[3,1536]{1,0:T(4,128)} %pos_ref.1, f32[3,1536]{1,0:T(4,128)} %vel_ref.1, f32[4,1536]{1,0:T(4,128)} %par_ref.1, s32[3,16896]{1,0:T(4,128)} %pl_in.1, ...), custom_call_target="tpu_custom_call" | custom-call | tf_op jit(solution)/shard_map/force_step/pallas_call | solution.py:410
  48.2 0.0 copy-done
  48.2 0.0 copy-done.1
  48.2 0.0 copy-done.2
  48.2 0.7 %update.1 = (f32[3,1536]{1,0:T(4,128)}, f32[3,1536]{1,0:T(4,128)}, f32[3,1536]{1,0:T(4,128)}, f32[4]{0:T(128)}) custom-call(f32[3,1536]{1,0:T(4,128)S(1)} %get-tuple-element.6.force_in, f32[8,128]{1,0:T(8,128)S(1)} %get-tuple-element.7.coef_ref, f32[3,1536]{1,0:T(4,128)S(1)} %copy-done, f32[3,1536]{1,0:T(4,128)S(1)} %copy-done.1, f32[4,1536]{1,0:T(4,128)S(1)} %copy-done.2), custom_call_target="tpu_custom_call" | custom-call | tf_op jit(solution)/shard_map/update/pallas_call | solution.py:466
Async XLA Ops:
  1.3 46.9 %copy-start = (f32[3,1536]{1,0:T(4,128)S(1)}, f32[3,1536]{1,0:T(4,128)}, u32[]{:S(2)}) copy-start(f32[3,1536]{1,0:T(4,128)} %pos_ref.1) | copy-start | bytes 55300
  1.3 46.9 %copy-start.1 = (f32[3,1536]{1,0:T(4,128)S(1)}, f32[3,1536]{1,0:T(4,128)}, u32[]{:S(2)}) copy-start(f32[3,1536]{1,0:T(4,128)} %vel_ref.1) | copy-start | bytes 55300
  1.3 46.9 %copy-start.2 = (f32[4,1536]{1,0:T(4,128)S(1)}, f32[4,1536]{1,0:T(4,128)}, u32[]{:S(2)}) copy-start(f32[4,1536]{1,0:T(4,128)} %par_ref.1) | copy-start | bytes 73732

commit v7 on v6

--- a/solution.py
+++ b/solution.py
@@ -130,7 +130,7 @@
         else:
             mix_out[c - 3] = jnp.where(lane8 < half, own[0], heads[c - 3])
     pl.semaphore_wait(barrier, len(greeted))
-    for item in halo_copies:
+    for item in (halo_copies[2], halo_copies[0], halo_copies[1]):
         item.start()
 
     def tell(round_, distance):

time: 49 us -> 48.6 us (level)
  no operation moved by 1% of the time
where the time goes in v7:
time: 48.6 us; the launch traced here: 48.4 us
  Pallas kernels  47.1 us (97%)
  between operations  1.33 us (3%)
    pallas_call x1, Pallas kernels, on_device(): pl.pallas_call(functools.partial(step_kernel, domains), out_shape=(rows,...  46.4 us

profile of v7, /device:TPU:40, one launch (start us, length us, event | category | flops | bytes accessed | tf_op | source)
XLA Modules:
  0.0 48.4 jit_solution(1640677005127680977)
XLA Ops:
  1.3 0.0 copy-start
  1.3 0.0 copy-start.1
  1.3 0.0 copy-start.2
  1.3 46.4 %force_step.1 = (f32[3,1536]{1,0:T(4,128)S(1)}, f32[8,128]{1,0:T(8,128)S(1)}) custom-call(s32[1]{0:T(128)S(6)} %copy.13.count_in, f32[3]{0:T(128)} %box_in.1, f32[4]{0:T(128)} %ext_in.1, s32[1,96]{1,0:T(1,128)} %bitcast.1, f32[3,1536]{1,0:T(4,128)} %pos_ref.1, f32[3,1536]{1,0:T(4,128)} %vel_ref.1, f32[4,1536]{1,0:T(4,128)} %par_ref.1, s32[3,16896]{1,0:T(4,128)} %pl_in.1, ...), custom_call_target="tpu_custom_call" | custom-call | tf_op jit(solution)/shard_map/force_step/pallas_call | solution.py:410
  47.8 0.0 copy-done
  47.8 0.0 copy-done.1
  47.8 0.0 copy-done.2
  47.8 0.7 %update.1 = (f32[3,1536]{1,0:T(4,128)}, f32[3,1536]{1,0:T(4,128)}, f32[3,1536]{1,0:T(4,128)}, f32[4]{0:T(128)}) custom-call(f32[3,1536]{1,0:T(4,128)S(1)} %get-tuple-element.6.force_in, f32[8,128]{1,0:T(8,128)S(1)} %get-tuple-element.7.coef_ref, f32[3,1536]{1,0:T(4,128)S(1)} %copy-done, f32[3,1536]{1,0:T(4,128)S(1)} %copy-done.1, f32[4,1536]{1,0:T(4,128)S(1)} %copy-done.2), custom_call_target="tpu_custom_call" | custom-call | tf_op jit(solution)/shard_map/update/pallas_call | solution.py:466
Async XLA Ops:
  1.3 46.5 %copy-start = (f32[3,1536]{1,0:T(4,128)S(1)}, f32[3,1536]{1,0:T(4,128)}, u32[]{:S(2)}) copy-start(f32[3,1536]{1,0:T(4,128)} %pos_ref.1) | copy-start | bytes 55300
  1.3 46.5 %copy-start.1 = (f32[3,1536]{1,0:T(4,128)S(1)}, f32[3,1536]{1,0:T(4,128)}, u32[]{:S(2)}) copy-start(f32[3,1536]{1,0:T(4,128)} %vel_ref.1) | copy-start | bytes 55300
  1.3 46.5 %copy-start.2 = (f32[4,1536]{1,0:T(4,128)S(1)}, f32[4,1536]{1,0:T(4,128)}, u32[]{:S(2)}) copy-start(f32[4,1536]{1,0:T(4,128)} %par_ref.1) | copy-start | bytes 73732

commit v8 on v7

--- a/solution.py
+++ b/solution.py
@@ -292,7 +292,7 @@
     plane_copies += [
         copy(src1, prev1.at[place], send3.at[k], recv3.at[place], above + lax.rem(place + k, PLANE))
         for k in range(PLANE)]
-    for item in plane_copies:
+    for item in plane_copies[PLANE - 1:] + plane_copies[:PLANE - 1]:
         item.start()
     dots(blocks - 1)
     tile_at = lambda k: acc_j[48 * k:48 * k + 24] + acc_j[48 * k + 24:48 * k + 48]

time: 48.6 us -> 48.7 us (level)
  no operation moved by 1% of the time
where the time goes in v8:
time: 48.7 us; the launch traced here: 48.5 us
  Pallas kernels  47.2 us (97%)
  between operations  1.33 us (3%)
    pallas_call x1, Pallas kernels, on_device(): pl.pallas_call(functools.partial(step_kernel, domains), out_shape=(rows,...  46.5 us

profile of v8, /device:TPU:40, one launch (start us, length us, event | category | flops | bytes accessed | tf_op | source)
XLA Modules:
  0.0 48.5 jit_solution(11002450640567380083)
XLA Ops:
  1.3 0.0 copy-start
  1.3 0.0 copy-start.1
  1.3 0.0 copy-start.2
  1.3 46.5 %force_step.1 = (f32[3,1536]{1,0:T(4,128)S(1)}, f32[8,128]{1,0:T(8,128)S(1)}) custom-call(s32[1]{0:T(128)S(6)} %copy.13.count_in, f32[3]{0:T(128)} %box_in.1, f32[4]{0:T(128)} %ext_in.1, s32[1,96]{1,0:T(1,128)} %bitcast.1, f32[3,1536]{1,0:T(4,128)} %pos_ref.1, f32[3,1536]{1,0:T(4,128)} %vel_ref.1, f32[4,1536]{1,0:T(4,128)} %par_ref.1, s32[3,16896]{1,0:T(4,128)} %pl_in.1, ...), custom_call_target="tpu_custom_call" | custom-call | tf_op jit(solution)/shard_map/force_step/pallas_call | solution.py:410
  47.9 0.0 copy-done
  47.9 0.0 copy-done.1
  47.9 0.0 copy-done.2
  47.9 0.7 %update.1 = (f32[3,1536]{1,0:T(4,128)}, f32[3,1536]{1,0:T(4,128)}, f32[3,1536]{1,0:T(4,128)}, f32[4]{0:T(128)}) custom-call(f32[3,1536]{1,0:T(4,128)S(1)} %get-tuple-element.6.force_in, f32[8,128]{1,0:T(8,128)S(1)} %get-tuple-element.7.coef_ref, f32[3,1536]{1,0:T(4,128)S(1)} %copy-done, f32[3,1536]{1,0:T(4,128)S(1)} %copy-done.1, f32[4,1536]{1,0:T(4,128)S(1)} %copy-done.2), custom_call_target="tpu_custom_call" | custom-call | tf_op jit(solution)/shard_map/update/pallas_call | solution.py:466
Async XLA Ops:
  1.3 46.6 %copy-start = (f32[3,1536]{1,0:T(4,128)S(1)}, f32[3,1536]{1,0:T(4,128)}, u32[]{:S(2)}) copy-start(f32[3,1536]{1,0:T(4,128)} %pos_ref.1) | copy-start | bytes 55300
  1.3 46.6 %copy-start.1 = (f32[3,1536]{1,0:T(4,128)S(1)}, f32[3,1536]{1,0:T(4,128)}, u32[]{:S(2)}) copy-start(f32[3,1536]{1,0:T(4,128)} %vel_ref.1) | copy-start | bytes 55300
  1.3 46.6 %copy-start.2 = (f32[4,1536]{1,0:T(4,128)S(1)}, f32[4,1536]{1,0:T(4,128)}, u32[]{:S(2)}) copy-start(f32[4,1536]{1,0:T(4,128)} %par_ref.1) | copy-start | bytes 73732
